TPU v7x, 32 devices: a whole 2x2x4 slice. The times are simulated.
32 devices in a mesh: pitch: 4 (over x, core), span: 8 (over z, y).
Axes of the slice: x: 2, y: 2, z: 4, core: 2. Of those that a mesh axis runs over, the one named last changes fastest.
Arguments:
- residual: float32 [5, 4, 64, 1024], P(None, None, 'span', 'pitch'), may hold values from -0.6 to 0.6
- inverse_diagonal: float32 [5, 5, 4, 64, 1024], P(None, None, None, 'span', 'pitch'), may hold values from -0.1 to 1, as said below
- prior_increment: float32 [5, 4, 64, 1024], P(None, None, 'span', 'pitch'), may hold values from -3 to 3
- coupling: float32 [6, 5, 5], replicated, may hold values from -1 to 1
- characteristic: float32 [2, 2, 512, 5, 5], replicated, may hold values from -6 to 6
- cutoffs: int32 [2], replicated, may hold values from 128 to 512
Outputs:
- update: float32 [5, 4, 64, 1024], P(None, None, 'span', 'pitch')
Inputs may be any that keep to these rules, and one draw needn't show every extreme that they name: `inverse_diagonal`: each cell's block is dominated by its diagonal; the sweeps' recurrences are stable.
All inputs are finite; a program needn't handle non-finite values.
Results may differ from a plain program's by a relative error of at most 0.0003.
Values sent between devices are 32-bit elements; how exact they have to be, the bound alone decides.
A program may use at most 64 MiB of HBM per device.

v0:
```python
import jax
import jax.numpy as jnp
import numpy as np
from jax import lax
from jax.experimental import pallas as pl
from jax.experimental.pallas import tpu as pltpu
from jax.sharding import PartitionSpec as P

highest = lax.Precision.HIGHEST
LANES = 128
VMEM = pltpu.VMEM
SMEM = pltpu.SMEM


def greet(axis):
    n = lax.axis_size(axis)
    me = lax.axis_index(axis)
    barrier = pltpu.get_barrier_semaphore()
    for step in range(1, n):
        pl.semaphore_signal(
            barrier,
            inc=1,
            device_id={axis: lax.rem(me + step, n)},
            device_id_type=pl.DeviceIdType.MESH,
        )


def greeted(axis):
    pl.semaphore_wait(pltpu.get_barrier_semaphore(), lax.axis_size(axis) - 1)


def start_exchange(source, target, send, recv, axis, gather):
    n = lax.axis_size(axis)
    me = lax.axis_index(axis)
    copies = []
    for step in range(1, n):
        to = lax.rem(me + step, n)
        copy = pltpu.make_async_remote_copy(
            src_ref=source if gather else source.at[to],
            dst_ref=target.at[me],
            send_sem=send.at[step - 1],
            recv_sem=recv.at[step - 1],
            device_id={axis: to},
            device_id_type=pl.DeviceIdType.MESH,
        )
        copy.start()
        copies.append(copy)
    return copies


def wait_all(copies):
    for copy in copies:
        copy.wait()


def semaphores(axis, exchanges):
    n = lax.axis_size(axis)
    return [pltpu.SemaphoreType.DMA((n - 1,)) for _ in range(2 * exchanges)]


def total(terms):
    result = terms[0]
    for term in terms[1:]:
        result = result + term
    return result


def scaled(block, matrix, nv):
    return [
        [-total([block[i][j] * matrix(j, k) for j in range(nv)]) for k in range(nv)]
        for i in range(nv)
    ]


def times(block, vector, nv):
    return [total([block[i][j] * vector[j] for j in range(nv)]) for i in range(nv)]


def load_block(diag, row, nv):
    return [[diag[i * nv + j, row] for j in range(nv)] for i in range(nv)]


def local_kernel(nv, coupling, diag, residual, neighbours, source, packed, maps, stars):
    rows = diag.shape[1]
    tile = diag.shape[2:]
    zero = jnp.zeros(tile, jnp.float32)
    one = jnp.ones(tile, jnp.float32)

    def entry(which):
        return lambda i, j: coupling[(which * nv + i) * nv + j]

    identity = [zero + (one if i == j else zero) for j in range(nv) for i in range(nv)]

    def column(flat, j):
        return flat[j * nv:(j + 1) * nv]

    def forward(row, carry):
        star, grown = list(carry[:nv]), list(carry[nv:])
        block = load_block(diag, row, nv)
        rhs = []
        for i in range(nv):
            value = residual[i, row]
            for side in range(4):
                matrix = entry(2 + side)
                for j in range(nv):
                    value = value - matrix(i, j) * neighbours[side * nv + j, row]
            source[i, row] = value
            rhs.append(value)
        step = scaled(block, entry(0), nv)
        star = [x + y for x, y in zip(times(block, rhs, nv), times(step, star, nv))]
        new = []
        for j in range(nv):
            new += times(step, column(grown, j), nv)
        for i in range(nv):
            stars[row, i] = star[i]
        for m in range(nv * nv):
            maps[row, m] = new[m]
        return tuple(star + new)

    last = lax.fori_loop(0, rows, forward, tuple([zero] * nv + identity))
    for m in range(nv + nv * nv):
        packed[m] = last[m]

    def backward(index, carry):
        row = rows - 1 - index
        nn = nv * nv
        base, response, grown = list(carry[:nv]), list(carry[nv:nv + nn]), list(carry[nv + nn:])
        step = scaled(load_block(diag, row, nv), entry(1), nv)
        base = [stars[row, i] + y for i, y in enumerate(times(step, base, nv))]
        new_response, new = [], []
        for j in range(nv):
            moved = times(step, column(response, j), nv)
            new_response += [maps[row, j * nv + i] + moved[i] for i in range(nv)]
            new += times(step, column(grown, j), nv)
        return tuple(base + new_response + new)

    initial = tuple([zero] * (nv + nv * nv) + identity)
    final = lax.fori_loop(0, rows, backward, initial)
    for m in range(nv + 2 * nv * nv):
        packed[nv + nv * nv + m] = final[m]


def solve_kernel(nv, got, out):
    n = got.shape[0]
    lanes = got.shape[2]
    nn = nv * nv

    def mapped(d, start, vector):
        return total(
            [
                got[d, start + j * nv:start + (j + 1) * nv, :] * vector[j:j + 1]
                for j in range(nv)
            ]
        )

    incoming = jnp.zeros((nv, lanes), jnp.float32)
    all_incoming = []
    for d in range(n):
        all_incoming.append(incoming)
        out[d, 0:nv, :] = incoming
        if d + 1 < n:
            incoming = got[d, 0:nv, :] + mapped(d, nv, incoming)
    following = jnp.zeros((nv, lanes), jnp.float32)
    base = nv + nn
    for d in reversed(range(n)):
        out[d, nv:2 * nv, :] = following
        if d > 0:
            known = got[d, base:base + nv, :] + mapped(d, base + nv, all_incoming[d])
            following = known + mapped(d, base + nv + nn, following)


def final_kernel(nv, coupling, diag, source, incoming, update, stars):
    rows = diag.shape[1]

    def mixed(which, vector):
        return [
            total([coupling[(which * nv + i) * nv + j] * vector[j] for j in range(nv)])
            for i in range(nv)
        ]

    def forward(row, star):
        pushed = mixed(0, star)
        rhs = [source[i, row] - pushed[i] for i in range(nv)]
        star = times(load_block(diag, row, nv), rhs, nv)
        for i in range(nv):
            stars[row, i] = star[i]
        return tuple(star)

    lax.fori_loop(0, rows, forward, tuple(incoming[i] for i in range(nv)))

    def backward(index, following):
        row = rows - 1 - index
        moved = times(load_block(diag, row, nv), mixed(1, following), nv)
        value = [stars[row, i] - moved[i] for i in range(nv)]
        for i in range(nv):
            update[i, row] = value[i]
        return tuple(value)

    lax.fori_loop(0, rows, backward, tuple(incoming[nv + i] for i in range(nv)))


def spectral_kernel(
    nv, rows, turns, cutoffs, x_ref, all_tables, entries, out, edges,
    got, parts, landed, table, picked, fetched, s0, r0, s1, r1
):
    n = lax.axis_size("pitch")
    me = lax.axis_index("pitch")
    flat = 2 * nv * rows
    greet("pitch")
    fetch = pltpu.make_async_copy(all_tables.at[me], table, fetched)
    fetch.start()
    got[me] = x_ref[...]
    turn = [turns[part * n * n + me * n + q] for part in range(2) for q in range(n)]
    harmonics = entries.shape[1]
    own = harmonics // n
    points = n * x_ref.shape[1]
    chosen = lax.broadcasted_iota(jnp.int32, (harmonics, own), 0) == (
        n * lax.broadcasted_iota(jnp.int32, (harmonics, own), 1) + me
    )
    picked[...] = jnp.dot(
        entries[...],
        jnp.where(chosen, 1.0, 0.0).astype(jnp.float32),
        precision=highest,
        preferred_element_type=jnp.float32,
    )
    mine = n * lax.broadcasted_iota(jnp.int32, (1, own), 1) + me
    weights = jnp.where(mine == 0, 1.0, 2.0).astype(jnp.float32) / points
    greeted("pitch")
    wait_all(start_exchange(x_ref, got, s0, r0, "pitch", True))
    fetch.wait()
    edges[...] = got[:, flat:, :]
    waves = total([got[q, :flat, :] * turn[q] for q in range(n)])
    waves_imag = -total([got[q, :flat, :] * turn[n + q] for q in range(n)])
    both = jnp.concatenate([waves, waves_imag])
    cosine, sine = table[0], table[1]
    with_cos = jnp.dot(both, cosine, precision=highest, preferred_element_type=jnp.float32)
    with_sin = jnp.dot(both, sine, precision=highest, preferred_element_type=jnp.float32)
    real_part = with_cos[:flat] + with_sin[flat:]
    imag_part = with_cos[flat:] - with_sin[:flat]
    out_real, out_imag = [], []
    for q in range(2):
        weight = jnp.where(mine < cutoffs[q], weights, 0.0)
        sr = [real_part[(q * nv + j) * rows:(q * nv + j + 1) * rows] for j in range(nv)]
        si = [imag_part[(q * nv + j) * rows:(q * nv + j + 1) * rows] for j in range(nv)]
        for i in range(nv):
            at = [((i * nv + j) * 2 + q) * 2 for j in range(nv)]
            cr = [picked[m:m + 1, :] for m in at]
            ci = [picked[m + 1:m + 2, :] for m in at]
            out_real.append(total([cr[j] * sr[j] - ci[j] * si[j] for j in range(nv)]) * weight)
            out_imag.append(total([cr[j] * si[j] + ci[j] * sr[j] for j in range(nv)]) * weight)
    stacked = jnp.concatenate(out_real + out_imag)

    def back(matrix):
        return lax.dot_general(
            stacked,
            matrix,
            (((1,), (1,)), ((), ())),
            precision=highest,
            preferred_element_type=jnp.float32,
        )

    with_cos, with_sin = back(cosine), back(sine)
    field = with_cos[:flat] - with_sin[flat:]
    field_imag = with_sin[:flat] + with_cos[flat:]
    for q in range(n):
        parts[q] = field * turn[q] - field_imag * turn[n + q]
    copies = start_exchange(parts, landed, s1, r1, "pitch", False)
    landed[me] = parts[me]
    wait_all(copies)
    out[...] = total([landed[q] for q in range(n)])


def sweeps_kernel(
    nv, coupling, diag, residual, neighbours, update,
    source, maps, stars, packed, send, got, solved, back, incoming, s0, r0, s1, r1
):
    n = lax.axis_size("span")
    me = lax.axis_index("span")
    share = send.shape[2]
    pieces = LANES // share
    greet("span")
    local_kernel(nv, coupling, diag, residual, neighbours, source, packed, maps, stars)
    for m in range(packed.shape[0]):
        value = packed[m]
        if pieces == 1:
            send[:, m, :] = value
        else:
            for d in range(n):
                lane = d % pieces * share
                row = d // pieces
                send[d, m:m + 1, :] = value[row:row + 1, lane:lane + share]
    greeted("span")
    copies = start_exchange(send, got, s0, r0, "span", False)
    got[me] = send[me]
    wait_all(copies)
    solve_kernel(nv, got, solved)
    copies = start_exchange(solved, back, s1, r1, "span", False)
    back[me] = solved[me]
    wait_all(copies)
    for m in range(2 * nv):
        if pieces == 1:
            incoming[m] = back[:, m, :]
        else:
            for d in range(n):
                lane = d % pieces * share
                row = d // pieces
                incoming[m, row:row + 1, lane:lane + share] = back[d, m:m + 1, :]
    final_kernel(nv, coupling, diag, source, incoming, update, stars)


def tables(n, width, harmonics):
    points = n * width
    own = harmonics // n
    k = n * np.arange(own)[None, :] + np.arange(n)[:, None]
    product = (np.arange(width)[None, :, None] * k[:, None, :]) % points
    angle = product * (2.0 * np.pi / points)
    return np.stack([np.cos(angle), np.sin(angle)], axis=1).astype(np.float32)


def corrections(residual, prior, characteristic, cutoffs):
    n = lax.axis_size("pitch")
    me = lax.axis_index("pitch")
    nv, _, rows, width = residual.shape
    harmonics = characteristic.shape[2]
    points = n * width
    own = harmonics // n
    flat_rows = 2 * nv * rows
    planes = jnp.stack([residual[:, 0], residual[:, -1]]).reshape(flat_rows, width)
    edges = jnp.stack([prior[..., 0], prior[..., -1]]).reshape(-1)
    edge_rows = -(-edges.shape[0] // width)
    edge_rows = -(-edge_rows // 8) * 8
    edges = jnp.pad(edges, (0, edge_rows * width - edges.shape[0])).reshape(edge_rows, width)
    turn = 2.0 * np.pi * (np.arange(n)[:, None] * np.arange(n)[None, :] % n) / n
    turns = jnp.asarray(np.concatenate([np.cos(turn), np.sin(turn)]).reshape(-1), jnp.float32)
    entries = characteristic.transpose(3, 4, 0, 1, 2).reshape(-1, harmonics)
    smem = pl.BlockSpec(memory_space=SMEM)
    vmem = pl.BlockSpec(memory_space=VMEM)
    total_rows = flat_rows + edge_rows
    correction, gathered = pl.pallas_call(
        lambda *refs: spectral_kernel(nv, rows, *refs),
        out_shape=(
            jax.ShapeDtypeStruct((flat_rows, width), jnp.float32),
            jax.ShapeDtypeStruct((n, edge_rows, width), jnp.float32),
        ),
        in_specs=[smem, smem, vmem, pl.BlockSpec(memory_space=pl.ANY), vmem],
        out_specs=(vmem, vmem),
        scratch_shapes=[
            VMEM((n, total_rows, width), jnp.float32),
            VMEM((n, flat_rows, width), jnp.float32),
            VMEM((n, flat_rows, width), jnp.float32),
            VMEM((2, width, own), jnp.float32),
            VMEM((entries.shape[0], own), jnp.float32),
            pltpu.SemaphoreType.DMA,
        ]
        + semaphores("pitch", 2),
        compiler_params=pltpu.CompilerParams(collective_id=0, has_side_effects=True),
        name="spectral",
    )(
        turns,
        cutoffs,
        jnp.concatenate([planes, edges]),
        jnp.asarray(tables(n, width, harmonics)),
        entries,
    )
    edge_shape = (2,) + prior.shape[:-1]
    count = int(np.prod(edge_shape))

    def edges_of(device):
        piece = lax.dynamic_index_in_dim(gathered, device, 0, keepdims=False)
        return piece.reshape(-1)[:count].reshape(edge_shape)

    before = edges_of(lax.rem(me + n - 1, n))[1][..., None]
    after = edges_of(lax.rem(me + 1, n))[0][..., None]

    return correction.reshape(2, nv, rows, width), before, after


def body(residual, inverse_diagonal, prior, coupling, characteristic, cutoffs):
    nv, axial, rows, width = residual.shape
    cells = axial * width
    tile = (cells // LANES, LANES)
    n = lax.axis_size("span")

    def by_row(field):
        lead = field.shape[:-3]
        return jnp.moveaxis(field, -2, -3).reshape((-1, rows) + tile)

    diag = by_row(inverse_diagonal)
    correction, before, after = corrections(residual, prior, characteristic, cutoffs)
    corrected = by_row(residual.at[:, 0].add(correction[0]).at[:, -1].add(correction[1]))
    blank = jnp.zeros_like(prior[:, :1])
    neighbours = by_row(
        jnp.stack(
            [
                jnp.concatenate([before, prior[..., :-1]], axis=3),
                jnp.concatenate([prior[..., 1:], after], axis=3),
                jnp.concatenate([blank, prior[:, :-1]], axis=1),
                jnp.concatenate([prior[:, 1:], blank], axis=1),
            ]
        )
    )
    scalars = coupling.reshape(-1)
    nn = nv * nv
    count = 2 * nv + 3 * nn
    smem = pl.BlockSpec(memory_space=SMEM)
    vmem = pl.BlockSpec(memory_space=VMEM)
    share = cells // n
    update = pl.pallas_call(
        lambda *refs: sweeps_kernel(nv, *refs),
        out_shape=jax.ShapeDtypeStruct((nv, rows) + tile, jnp.float32),
        in_specs=[smem, vmem, vmem, vmem],
        out_specs=vmem,
        scratch_shapes=[
            VMEM((nv, rows) + tile, jnp.float32),
            VMEM((rows, nn) + tile, jnp.float32),
            VMEM((rows, nv) + tile, jnp.float32),
            VMEM((count,) + tile, jnp.float32),
            VMEM((n, count, share), jnp.float32),
            VMEM((n, count, share), jnp.float32),
            VMEM((n, 2 * nv, share), jnp.float32),
            VMEM((n, 2 * nv, share), jnp.float32),
            VMEM((2 * nv,) + tile, jnp.float32),
        ]
        + semaphores("span", 2),
        compiler_params=pltpu.CompilerParams(collective_id=1, has_side_effects=True),
        name="sweeps",
    )(scalars, diag, corrected, neighbours)
    return jnp.moveaxis(update.reshape(nv, rows, axial, width), 1, 2)


def solution(mesh):
    in_specs = (
        P(None, None, "span", "pitch"),
        P(None, None, None, "span", "pitch"),
        P(None, None, "span", "pitch"),
        P(),
        P(),
        P(),
    )
    out_specs = P(None, None, "span", "pitch")
    return jax.shard_map(body, mesh=mesh, in_specs=in_specs, out_specs=out_specs, check_vma=False)
```

profile of v0, /device:TPU:0, one launch (start us, length us, event | category | flops | bytes accessed | tf_op | source)
XLA Modules:
  0.0 50.6 jit_solution(9699590126798344784)
XLA Ops:
  0.0 0.9 %copy.37 = f32[5,4,8,256]{3,2,1,0:T(8,128)S(1)} copy(f32[5,4,8,256]{3,2,1,0:T(8,128)} %param.12) | data formatting | bytes 327680
  0.9 0.0 copy-done.3
  0.9 0.7 %reshape.120.refs_0_ = f32[150]{0:T(256)} reshape(f32[6,5,5]{2,1,0:T(8,128)S(1)} %copy.18) | data formatting | bytes 1200 | tf_op jit(solution)/shard_map/reshape | solution.py:402
  1.6 1.5 %copy.19 = f32[5,5,8,4,256]{4,3,2,1,0:T(4,128)S(1)} copy(f32[5,5,8,4,256]{4,2,3,1,0:T(8,128)} %bitcast.38) | data formatting | bytes 1638400 | tf_op jit(solution)/shard_map/transpose | solution.py:386
  3.1 0.0 copy-start
  3.1 1.2 %reshape.121.refs_1_ = f32[25,8,8,128]{3,2,1,0:T(8,128)} reshape(f32[5,5,8,4,256]{4,3,2,1,0:T(4,128)S(1)} %copy.19) | data formatting | bytes 1638400 | tf_op jit(solution)/shard_map/reshape | solution.py:386
  4.3 0.0 copy-done
  4.3 0.2 fusion.4
  4.5 0.2 copy.31
  4.7 0.1 reshape.123
  4.9 0.0 copy-start.1
  4.9 0.6 %pad_maximum_fusion.refs_2_ = f32[88,256]{1,0:T(8,128)} fusion(f32[8,256]{1,0:T(8,128)S(1)} %reshape.124, f32[80,256]{1,0:T(8,128)S(1)} %bitcast.39), kind=kLoop, calls=%fused_computation.6 | loop fusion | flops 22528 | bytes 180224 | tf_op jit(solution)/shard_map/concatenate | solution.py:361
  5.5 0.3 copy-done.1
  5.9 0.8 %reshape.125.refs_4_ = f32[100,512]{1,0:T(8,128)} reshape(f32[5,5,2,2,512]{4,3,2,1,0:T(2,128)S(1)} %copy.22) | data formatting | bytes 409600 | tf_op jit(solution)/shard_map/reshape | solution.py:335
  6.7 15.4 %spectral.1 = (f32[80,256]{1,0:T(8,128)}, f32[4,8,256]{2,1,0:T(8,128)}) custom-call(f32[32]{0:T(128)} %constant.84.clone.refs_0_, s32[2]{0:T(128)} %refs_1_.1, f32[88,256]{1,0:T(8,128)} %pad_maximum_fusion.refs_2_, f32[4,2,256,128]{3,2,1,0:T(8,128)} %constant.85.clone.refs_3_, f32[100,512]{1,0:T(8,128)} %reshape.125.refs_4_), custom_call_target="tpu_custom_call" | custom-call | tf_op jit(solution)/shard_map/spectral/pallas_call | solution.py:339
  22.1 0.0 copy-start.2
  22.1 0.9 %fusion.1 = f32[5,4,8,256]{3,2,1,0:T(8,128)S(1)} fusion(f32[5,4,8,256]{3,2,1,0:T(8,128)S(1)} %copy.37, f32[80,256]{1,0:T(8,128)} %get-tuple-element.31), kind=kLoop, calls=%fused_computation.12 | loop fusion | flops 10240 | bytes 122880 | tf_op jit(solution)/shard_map/scatter-add | solution.py:390
  22.9 0.0 copy-done.2
  23.0 0.1 copy.25
  23.0 0.7 %reshape.128.refs_2_ = f32[5,8,8,128]{3,2,1,0:T(8,128)} reshape(f32[5,8,4,256]{3,2,1,0:T(4,128)S(1)} %copy.25) | data formatting | bytes 327680 | tf_op jit(solution)/shard_map/reshape | solution.py:386
  23.8 0.1 fusion.2
  24.0 0.7 %copy-done.4 = f32[4,8,256]{2,1,0:T(8,128)S(1)} copy-done((f32[4,8,256]{2,1,0:T(8,128)S(1)}, f32[4,8,256]{2,1,0:T(8,128)}, u32[]{:S(2)}) %copy-start.4) | copy-done | bytes 32792
  24.7 0.2 slice.111
  24.9 0.2 copy.26
  25.1 0.2 slice.115
  25.3 0.2 copy.27
  25.5 0.1 maximum_bitcast_fusion.1
  25.7 0.3 copy.28
  26.0 1.1 %reshape.129.refs_3_ = f32[20,8,8,128]{3,2,1,0:T(8,128)} reshape(f32[4,5,8,4,256]{4,3,2,1,0:T(4,128)S(1)} %copy.28) | data formatting | bytes 1310720 | tf_op jit(solution)/shard_map/reshape | solution.py:386
  27.1 21.8 %sweeps.1 = f32[5,8,8,128]{3,2,1,0:T(8,128)} custom-call(f32[150]{0:T(256)} %reshape.120.refs_0_, f32[25,8,8,128]{3,2,1,0:T(8,128)} %reshape.121.refs_1_, f32[5,8,8,128]{3,2,1,0:T(8,128)} %reshape.128.refs_2_, f32[20,8,8,128]{3,2,1,0:T(8,128)} %reshape.129.refs_3_), custom_call_target="tpu_custom_call" | custom-call | tf_op jit(solution)/shard_map/sweeps/pallas_call | solution.py:408
  48.9 1.0 %reshape.130 = f32[5,8,4,256]{3,2,1,0:T(4,128)S(1)} reshape(f32[5,8,8,128]{3,2,1,0:T(8,128)} %sweeps.1) | data formatting | bytes 327680 | tf_op jit(solution)/shard_map/reshape | solution.py:428
  49.9 0.7 %copy.33 = f32[5,8,4,256]{3,1,2,0:T(8,128)} copy(f32[5,8,4,256]{3,2,1,0:T(4,128)S(1)} %reshape.130) | data formatting | bytes 327680 | tf_op jit(solution)/shard_map/reshape | solution.py:428
  (16 shorter events, 0.2 us)
Async XLA Ops:
  0.0 0.9 %copy-start.3 = (f32[6,5,5]{2,0,1:T(8,128)S(1)}, f32[6,5,5]{2,0,1:T(8,128)}, u32[]{:S(2)}) copy-start(f32[6,5,5]{2,0,1:T(8,128)} %param.15) | copy-start | bytes 1804
  3.1 1.2 %copy-start = (f32[5,4,8,256]{3,2,1,0:T(8,128)S(1)}, f32[5,4,8,256]{3,2,1,0:T(8,128)}, u32[]{:S(2)}) copy-start(f32[5,4,8,256]{3,2,1,0:T(8,128)} %param.14) | copy-start | bytes 491524
  4.9 1.0 %copy-start.1 = (f32[2,2,512,5,5]{2,1,4,3,0:T(2,128)S(1)}, f32[2,2,512,5,5]{2,1,4,3,0:T(2,128)}, u32[]{:S(2)}) copy-start(f32[2,2,512,5,5]{2,1,4,3,0:T(2,128)} %param.16) | copy-start | bytes 614404
  22.1 0.9 %copy-start.2 = (f32[80,256]{1,0:T(8,128)S(1)}, f32[80,256]{1,0:T(8,128)}, u32[]{:S(2)}) copy-start(f32[80,256]{1,0:T(8,128)} %get-tuple-element.31) | copy-start | bytes 245764
  23.9 0.8 %copy-start.4 = (f32[4,8,256]{2,1,0:T(8,128)S(1)}, f32[4,8,256]{2,1,0:T(8,128)}, u32[]{:S(2)}) copy-start(f32[4,8,256]{2,1,0:T(8,128)} %get-tuple-element.32) | copy-start | bytes 98308
where the time goes:
time: 51 us; the launch traced here: 50.6 us
  Pallas kernels  37.2 us (73%)
  local copies, waits for them, and re-layouts  11.5 us (23%)
  other arithmetic  1.71 us (3%)
    pallas_call x1, Pallas kernels, body(): pl.pallas_call(lambda *refs: sweeps_kernel(nv, *refs), out_shape=jax.Shap...  21.8 us
    pallas_call x1, Pallas kernels, corrections(): pl.pallas_call(lambda *refs: spectral_kernel(nv, rows, *refs), out_shape=...  15.4 us
    reshape x3, local copies, waits for them, and re-layouts, by_row(): return jnp.moveaxis(field, -2, -3).reshape((-1, rows) + tile)  3.07 us
    unnamed x13, local copies, waits for them, and re-layouts  2.18 us
    transpose x3, local copies, waits for them, and re-layouts, by_row(): return jnp.moveaxis(field, -2, -3).reshape((-1, rows) + tile)  1.79 us
    reshape x2, local copies, waits for them, and re-layouts, body(): return jnp.moveaxis(update.reshape(nv, rows, axial, width), 1, 2)  1.69 us

commit v1 on v0

v1 whole, which is shorter than its diff:
```python
import jax
import jax.numpy as jnp
import numpy as np
from jax import lax
from jax.experimental import pallas as pl
from jax.experimental.pallas import tpu as pltpu
from jax.sharding import PartitionSpec as P

LANES = 128
SUBLANES = 8
VMEM = pltpu.VMEM
SMEM = pltpu.SMEM
DMA = pltpu.SemaphoreType.DMA
MAPS = 80
EARLY = 88
PAIR = 16
F32 = jnp.float32
BF16 = jnp.bfloat16


def total(terms):
    result = terms[0]
    for term in terms[1:]:
        result = result + term
    return result


def tree(terms):
    while len(terms) > 1:
        terms = [
            terms[i] + terms[i + 1] if i + 1 < len(terms) else terms[i]
            for i in range(0, len(terms), 2)
        ]
    return terms[0]


def times(block, vector, nv):
    return [tree([block[i][j] * vector[j] for j in range(nv)]) for i in range(nv)]


def remote(src, dst, send, recv, device):
    return pltpu.make_async_remote_copy(
        src_ref=src,
        dst_ref=dst,
        send_sem=send,
        recv_sem=recv,
        device_id=device,
        device_id_type=pl.DeviceIdType.MESH,
    )


def split_dot(value, high, low):
    rows = value.shape[0]
    head = value.astype(BF16)
    rest = (value - head.astype(F32)).astype(BF16)
    both = jnp.dot(jnp.concatenate([head, rest]), high, preferred_element_type=F32)
    return both[:rows] + both[rows:] + jnp.dot(head, low, preferred_element_type=F32)


def tables(points, harmonics):
    quarter = points // 4
    p = np.arange(quarter)[:, None]
    blocks = []
    for s in range(4):
        angle = (p * (4 * np.arange(harmonics // 4)[None, :] + s) % points) * (2.0 * np.pi / points)
        blocks.append(np.concatenate([np.cos(angle), np.sin(angle)], axis=1))
    full = np.concatenate(blocks, axis=1).astype(np.float32)
    high = full.astype(BF16)
    low = (full - high.astype(np.float32)).astype(BF16)
    forward = np.stack([high, low])
    return forward, np.ascontiguousarray(forward.transpose(0, 2, 1))


def kernel(
    nv, axial, rows, cw, harmonics,
    cutoffs, coupling, res_in, prior_in, diag_in, char_in, fwd_in, inv_in,
    out,
    res, prior, diag, char, fwd, inv,
    stage, lines, edge, edges, entries, chars,
    low_steps, up_steps, grown, src, base, send_maps, send_pair,
    got_late, got_early, got_pair, solved_early, solved_late, back,
    corr_send, corr_got,
    in_sem, line_send, line_recv, edge_send, edge_recv, corr_ssem, corr_rsem,
    late_send, late_recv, early_send, early_recv, pair_send, pair_recv,
    re_send, re_recv, rl_send, rl_recv,
):
    n = lax.axis_size("pitch")
    m = lax.axis_size("span")
    me = lax.axis_index("pitch")
    mine = lax.axis_index("span")
    core = lax.rem(me, 2)
    chip = me // 2
    cells = axial * cw
    nn = nv * nv
    half = rows // 2
    count = nv * 2 * half
    owners = 2 * cw
    first = m // 2 - owners // 2
    own = mine - first
    is_owner = jnp.logical_and(own >= 0, own < owners)

    def late_row(k):
        return jnp.where(k < cw, k, cells - 2 * cw + k) if not isinstance(k, int) else (
            k if k < cw else cells - 2 * cw + k)

    def early_row(k):
        return cw + k

    copies = [
        pltpu.make_async_copy(a, b, in_sem.at[i])
        for i, (a, b) in enumerate(
            [(res_in, res), (prior_in, prior), (diag_in, diag), (char_in, char),
             (fwd_in, fwd), (inv_in, inv)]
        )
    ]
    for copy in copies:
        copy.start()
    get_res, get_prior, get_diag, get_char, get_fwd, get_inv = copies

    barrier = pltpu.get_barrier_semaphore()

    def greet(axis, to):
        pl.semaphore_signal(
            barrier, inc=1, device_id={axis: to}, device_id_type=pl.DeviceIdType.MESH
        )

    for step in range(1, n):
        greet("pitch", lax.rem(me + step, n))

    @pl.when(is_owner)
    def _():
        for step in range(1, m):
            greet("span", lax.rem(mine + step, m))

    @pl.when(jnp.logical_not(is_owner))
    def _():
        for k in range(owners):
            greet("span", first + k)

    def tile(ref, i, a, c):
        at = ((i * axial + a) * cw + c) * rows
        return ref[at:at + rows, :]

    get_res.wait()
    for h in range(2):
        for c in range(cw):
            for i in range(nv):
                for q in range(2):
                    a = 0 if q == 0 else axial - 1
                    at = ((i * axial + a) * cw + c) * rows + h * half
                    to = c * count + i * 2 * half + q * half
                    stage[h, to:to + half, :] = res[at:at + half, :]

    get_prior.wait()
    lane = lax.broadcasted_iota(jnp.int32, (rows, LANES), 1)
    packed = jnp.zeros((rows, LANES), F32)
    for j in range(nv):
        for a in range(axial):
            at = j * axial + a
            left = jnp.broadcast_to(tile(prior, j, a, 0)[:, 0:1], (rows, LANES))
            right = jnp.broadcast_to(tile(prior, j, a, cw - 1)[:, LANES - 1:], (rows, LANES))
            packed = jnp.where(lane == at, left, packed)
            packed = jnp.where(lane == nv * axial + at, right, packed)
    edge[...] = packed

    @pl.when(is_owner)
    def _():
        pl.semaphore_wait(barrier, n - 1 + m - 1)

    @pl.when(jnp.logical_not(is_owner))
    def _():
        pl.semaphore_wait(barrier, n - 1 + owners)

    gather = []
    for step in [s for s in range(2, n)] + [1]:
        to = jnp.bitwise_xor(me, step)
        gather.append(
            remote(
                stage.at[lax.rem(to, 2)], lines.at[me], line_send.at[step - 1],
                line_recv.at[step - 1], {"pitch": to},
            )
        )
        gather[-1].start()
    after = lax.rem(me + 1, n)
    before = lax.rem(me + n - 1, n)
    edge_copies = [
        remote(edge, edges.at[0], edge_send.at[0], edge_recv.at[0], {"pitch": after}),
        remote(edge, edges.at[1], edge_send.at[1], edge_recv.at[1], {"pitch": before}),
    ]
    for copy in edge_copies:
        copy.start()
    lines[me] = stage[core]

    get_diag.wait()
    zero = jnp.zeros((cells, LANES), F32)
    one = jnp.ones((cells, LANES), F32)
    identity = [one if i == j else zero for j in range(nv) for i in range(nv)]

    def cell_row(ref, at, row):
        return ref[pl.ds(at * cells * rows + row, cells, stride=rows), :]

    def block_at(row):
        return [[cell_row(diag, i * nv + j, row) for j in range(nv)] for i in range(nv)]

    def entry(which, i, j):
        return coupling[(which * nv + i) * nv + j]

    def steps_at(ref, row):
        return [[ref[row, i * nv + j] for j in range(nv)] for i in range(nv)]

    def advance(ref, row, carry):
        step = steps_at(ref, row)
        new = []
        for j in range(nv):
            new += times(step, carry[j * nv:(j + 1) * nv], nv)
        return new

    def prepare(row, carry):
        block = block_at(row)
        for ref, which in ((low_steps, 0), (up_steps, 1)):
            for k in range(nv):
                column = [-entry(which, j, k) for j in range(nv)]
                for i in range(nv):
                    ref[row, i * nv + k] = tree([block[i][j] * column[j] for j in range(nv)])
        return carry

    lax.fori_loop(0, rows, prepare, 0)

    def grow(row, carry):
        new = advance(low_steps, row, list(carry))
        for at in range(nn):
            grown[row, at] = new[at]
        return tuple(new)

    last = lax.fori_loop(0, rows, grow, tuple(identity))
    for at in range(nn):
        send_maps[pl.ds(at, cells, stride=EARLY), :] = last[at]

    def respond(index, carry):
        row = rows - 1 - index
        new = advance(up_steps, row, list(carry))
        return tuple(grown[row, at] + new[at] for at in range(nn))

    response = lax.fori_loop(0, rows, respond, tuple([zero] * nn))
    for at in range(nn):
        send_maps[pl.ds(nn + at, cells, stride=EARLY), :] = response[at]

    def shrink(index, carry):
        return tuple(advance(up_steps, rows - 1 - index, list(carry)))

    last = lax.fori_loop(0, rows, shrink, tuple(identity))
    for at in range(nn):
        send_maps[pl.ds(2 * nn + at, cells, stride=EARLY), :] = last[at]

    def to_owners(make):
        for k in range(owners):
            @pl.when(mine != first + k)
            def _(k=k):
                make(k).start()

    def late_copy(k):
        return remote(
            send_maps.at[pl.ds(late_row(k) * EARLY, MAPS), :], got_late.at[mine],
            late_send.at[k], late_recv.at[mine], {"span": first + k},
        )

    def early_copy(k):
        return remote(
            send_maps.at[pl.ds(early_row(k) * EARLY, EARLY), :], got_early.at[mine],
            early_send.at[k], early_recv.at[mine], {"span": first + k},
        )

    def pair_copy(k):
        return remote(
            send_pair.at[pl.ds(late_row(k) * PAIR, PAIR), :], got_pair.at[mine],
            pair_send.at[k], pair_recv.at[mine], {"span": first + k},
        )

    for copy in edge_copies:
        copy.wait_recv()
    from_left, from_right = edges[0], edges[1]
    for a in range(axial):
        for c in range(cw):
            groups = [[], [], [], []]
            for j in range(nv):
                at = j * axial + a
                here = tile(prior, j, a, c)
                if c > 0:
                    border = pltpu.roll(tile(prior, j, a, c - 1), 1, 1)
                else:
                    border = pltpu.roll(from_left, LANES - (nv * axial + at), 1)
                groups[0].append(jnp.where(lane == 0, border, pltpu.roll(here, 1, 1)))
                if c + 1 < cw:
                    border = pltpu.roll(tile(prior, j, a, c + 1), LANES - 1, 1)
                else:
                    border = pltpu.roll(from_right, LANES - 1 - at, 1)
                groups[1].append(
                    jnp.where(lane == LANES - 1, border, pltpu.roll(here, LANES - 1, 1)))
                if a > 0:
                    groups[2].append(tile(prior, j, a - 1, c))
                if a + 1 < axial:
                    groups[3].append(tile(prior, j, a + 1, c))
            for i in range(nv):
                value = tile(res, i, a, c)
                for side in range(4):
                    for j, neighbour in enumerate(groups[side]):
                        value = value - entry(2 + side, i, j) * neighbour
                at = ((i * axial + a) * cw + c) * rows
                src[at:at + rows, :] = value

    def forward(row, star):
        block = block_at(row)
        rhs = [cell_row(src, i, row) for i in range(nv)]
        known = times(block, rhs, nv)
        for i in range(nv):
            base[row, i] = known[i]
        moved = times(steps_at(low_steps, row), list(star), nv)
        star = [x + y for x, y in zip(known, moved)]
        for i in range(nv):
            grown[row, i] = star[i]
        return tuple(star)

    def backward(index, following):
        row = rows - 1 - index
        moved = times(steps_at(up_steps, row), list(following), nv)
        return tuple(grown[row, i] + moved[i] for i in range(nv))

    def local_sweeps():
        last = lax.fori_loop(0, rows, forward, tuple([zero] * nv))
        top = lax.fori_loop(0, rows, backward, tuple([zero] * nv))
        return list(last) + list(top)

    ends = local_sweeps()
    for at in range(2 * nv):
        send_maps[pl.ds(3 * nn + at, cells, stride=EARLY), :] = ends[at]
    to_owners(late_copy)
    to_owners(early_copy)

    get_char.wait()
    for at in range(2 * nn):
        entries[2 * at:2 * at + 2, :] = char[at]
    table = entries[...]
    part = harmonics // 4
    source_k = lax.broadcasted_iota(jnp.int32, (harmonics, harmonics), 0)
    target = lax.broadcasted_iota(jnp.int32, (harmonics, harmonics), 1)
    wanted = 4 * lax.rem(target, part) + target // part
    chosen = jnp.where(source_k == wanted, 1.0, 0.0).astype(BF16)
    picked = jnp.zeros(table.shape, F32)
    rest = table
    for _ in range(3):
        head = rest.astype(BF16)
        rest = rest - head.astype(F32)
        picked = picked + jnp.dot(head, chosen, preferred_element_type=F32)
    entries[...] = picked
    points = n * cw * LANES
    upper = lax.broadcasted_iota(jnp.int32, (2 * half, part), 0) >= half
    index = lax.broadcasted_iota(jnp.int32, (2 * half, part), 1)
    for s in range(4):
        k = 4 * index + s
        weight = jnp.where(k == 0, 1.0, 2.0).astype(F32) / points
        kept = jnp.where(upper, cutoffs[1], cutoffs[0])
        weight = jnp.where(k < kept, weight, 0.0)
        for i in range(nv):
            for j in range(nv):
                for p in range(2):
                    at0 = 2 * (i * nv + j) + p
                    at1 = at0 + 2 * nn
                    a = jnp.broadcast_to(entries[at0:at0 + 1, s * part:(s + 1) * part],
                                         (2 * half, part))
                    b = jnp.broadcast_to(entries[at1:at1 + 1, s * part:(s + 1) * part],
                                         (2 * half, part))
                    chars[s, 2 * (i * nv + j) + p] = jnp.where(upper, b, a) * weight

    get_fwd.wait()
    for copy in gather:
        copy.wait_recv()
    per_quarter = (points // 4) // LANES
    quarters = []
    for q in range(4):
        pieces = []
        for t in range(q * per_quarter, (q + 1) * per_quarter):
            d, c = t // cw, t % cw
            pieces.append(lines[d, c * count:(c + 1) * count, :])
        quarters.append(jnp.concatenate(pieces, axis=1))
    even0, even1 = quarters[0] + quarters[2], quarters[1] + quarters[3]
    odd0, odd1 = quarters[0] - quarters[2], quarters[1] - quarters[3]
    wide = 2 * part

    def onward(value, s):
        return split_dot(
            value, fwd[0, :, s * wide:(s + 1) * wide], fwd[1, :, s * wide:(s + 1) * wide])

    real, imag = [None] * 4, [None] * 4
    for s, value in ((0, even0 + even1), (2, even0 - even1)):
        both = onward(value, s)
        real[s], imag[s] = both[:, :part], -both[:, part:]
    odd = jnp.concatenate([odd0, odd1])
    both = onward(odd, 1)
    real[1] = both[:count, :part] - both[count:, part:]
    imag[1] = -(both[:count, part:] + both[count:, :part])
    both = onward(odd, 3)
    real[3] = both[:count, :part] + both[count:, part:]
    imag[3] = both[count:, :part] - both[:count, part:]

    new_real, new_imag = [], []
    group = 2 * half
    for s in range(4):
        sr = [real[s][j * group:(j + 1) * group] for j in range(nv)]
        si = [imag[s][j * group:(j + 1) * group] for j in range(nv)]
        outr, outi = [], []
        for i in range(nv):
            cr = [chars[s, 2 * (i * nv + j)] for j in range(nv)]
            ci = [chars[s, 2 * (i * nv + j) + 1] for j in range(nv)]
            outr.append(total([cr[j] * sr[j] - ci[j] * si[j] for j in range(nv)]))
            outi.append(total([cr[j] * si[j] + ci[j] * sr[j] for j in range(nv)]))
        new_real.append(jnp.concatenate(outr))
        new_imag.append(jnp.concatenate(outi))

    get_inv.wait()

    def homeward(value, s):
        return split_dot(
            value, inv[0, s * wide:(s + 1) * wide, :], inv[1, s * wide:(s + 1) * wide, :])

    def beside(a, b):
        return jnp.concatenate([a, b], axis=1)

    r0 = homeward(beside(new_real[0], -new_imag[0]), 0)
    r2 = homeward(beside(new_real[2], -new_imag[2]), 2)
    both1 = homeward(
        jnp.concatenate(
            [beside(new_real[1], -new_imag[1]), beside(-new_imag[1], -new_real[1])]), 1)
    both3 = homeward(
        jnp.concatenate(
            [beside(new_real[3], -new_imag[3]), beside(new_imag[3], new_real[3])]), 3)
    odd_real = both1[:count] + both3[:count]
    odd_imag = both1[count:] + both3[count:]
    spans = (2 * cw) // per_quarter
    if spans == 2:
        sign = (1 - 2 * chip).astype(F32)
        fields = [r0 + r2 + sign * odd_real, r0 - r2 + sign * odd_imag]
    else:
        sign = (1 - 2 * (chip // 2)).astype(F32)
        turned = lax.rem(chip, 2).astype(F32)
        straight = 1.0 - turned
        field = r0 + (straight - turned) * r2 + sign * (
            straight * odd_real + turned * odd_imag)
        fields = [field[:, c * cw * LANES:(c + 1) * cw * LANES] for c in range(2)]
    is_first = core == 0
    for c in range(cw):
        lo, hi = c * LANES, (c + 1) * LANES
        a, b = fields[0][:, lo:hi], fields[1][:, lo:hi]
        corr_send[c * count:(c + 1) * count, :] = jnp.where(is_first, b, a)
        corr_got[0, c * count:(c + 1) * count, :] = jnp.where(is_first, a, b)
    swap = remote(
        corr_send, corr_got.at[1], corr_ssem, corr_rsem, {"pitch": jnp.bitwise_xor(me, 1)})
    swap.start()
    swap.wait_recv()
    lower_rows = lax.broadcasted_iota(jnp.int32, (rows, LANES), 0) < half
    for c in range(cw):
        for i in range(nv):
            for q in range(2):
                a = 0 if q == 0 else axial - 1
                at = ((i * axial + a) * cw + c) * rows
                fr = c * count + i * group + q * half
                ours = corr_got[0, fr:fr + half, :]
                theirs = corr_got[1, fr:fr + half, :]
                src[at:at + half, :] += jnp.where(is_first, ours, theirs)
                src[at + half:at + rows, :] += jnp.where(is_first, theirs, ours)

    ends = local_sweeps()
    for at in range(2 * nv):
        send_pair[pl.ds(at, cells, stride=PAIR), :] = ends[at]
    to_owners(pair_copy)

    def solve(maps, terms, offset, solved):
        def mapped(d, start, vector):
            return tree(
                [maps[d, start + j * nv:start + (j + 1) * nv, :] * vector[j:j + 1]
                 for j in range(nv)])

        def term(d, which):
            return terms[d, offset + which * nv:offset + (which + 1) * nv, :]

        incoming = jnp.zeros((nv, LANES), F32)
        every = []
        for d in range(m):
            every.append(incoming)
            solved[d, 0:nv, :] = incoming
            if d + 1 < m:
                incoming = term(d, 0) + mapped(d, 0, incoming)
        following = jnp.zeros((nv, LANES), F32)
        for d in reversed(range(m)):
            solved[d, nv:2 * nv, :] = following
            if d > 0:
                known = term(d, 1) + mapped(d, nn, every[d])
                following = known + mapped(d, 2 * nn, following)

    def reply(solved, row, send, recv):
        out_copies = []
        for step in range(1, m):
            to = lax.rem(mine + step, m)
            out_copies.append(
                remote(
                    solved.at[to], back.at[pl.ds(pl.multiple_of(row * PAIR, 8), PAIR), :],
                    send.at[step - 1], recv.at[own], {"span": to}))
            out_copies[-1].start()
        back[pl.ds(pl.multiple_of(row * PAIR, 8), PAIR), :] = solved[mine]
        return out_copies

    def arrived(make_buffer, recv):
        for step in range(1, m):
            d = lax.rem(mine + step, m)
            remote(
                make_buffer.at[d], make_buffer.at[d], recv.at[d], recv.at[d], {"span": d}
            ).wait_recv()

    def own_rows(ref, row, stride, size):
        return ref[pl.ds(pl.multiple_of(row * stride, 8), size), :]

    @pl.when(is_owner)
    def _():
        late = late_row(own)
        early = early_row(own)
        got_early[mine] = own_rows(send_maps, early, EARLY, EARLY)
        got_late[mine] = own_rows(send_maps, late, EARLY, MAPS)
        got_pair[mine] = own_rows(send_pair, late, PAIR, PAIR)
        arrived(got_early, early_recv)
        solve(got_early, got_early, 3 * nn, solved_early)
        first_out = reply(solved_early, early, re_send, re_recv)
        arrived(got_late, late_recv)
        arrived(got_pair, pair_recv)
        solve(got_late, got_pair, 0, solved_late)
        second_out = reply(solved_late, late, rl_send, rl_recv)
        for copy in first_out + second_out:
            copy.wait_send()

    for k in range(owners):
        @pl.when(mine != first + k)
        def _(k=k):
            for row, recv in ((early_row(k), re_recv), (late_row(k), rl_recv)):
                place = back.at[pl.ds(row * PAIR, PAIR), :]
                remote(place, place, recv.at[k], recv.at[k], {"span": first + k}).wait_recv()

    incoming = [back[pl.ds(i, cells, stride=PAIR), :] for i in range(2 * nv)]

    def last_forward(row, star):
        moved = times(steps_at(low_steps, row), list(star), nv)
        star = [base[row, i] + moved[i] for i in range(nv)]
        for i in range(nv):
            grown[row, i] = star[i]
        return tuple(star)

    def last_backward(index, following):
        row = rows - 1 - index
        value = backward(index, following)
        for i in range(nv):
            out[pl.ds(i * cells * rows + row, cells, stride=rows), :] = value[i]
        return value

    lax.fori_loop(0, rows, last_forward, tuple(incoming[:nv]))
    lax.fori_loop(0, rows, last_backward, tuple(incoming[nv:]))

    for copy in gather + edge_copies + [swap]:
        copy.wait_send()
    for k in range(owners):
        @pl.when(mine != first + k)
        def _(k=k):
            for make in (late_copy, early_copy, pair_copy):
                make(k).wait_send()


def body(residual, inverse_diagonal, prior, coupling, characteristic, cutoffs):
    nv, axial, rows, width = residual.shape
    n = lax.axis_size("pitch")
    m = lax.axis_size("span")
    cw = width // LANES
    cells = axial * cw
    nn = nv * nv
    harmonics = characteristic.shape[2]
    points = n * width
    owners = 2 * cw
    half = rows // 2
    count = 2 * nv * half
    part = harmonics // 4

    def flat(field):
        field = field.reshape(field.shape[:-1] + (cw, LANES))
        return jnp.swapaxes(field, -2, -3).reshape(-1, LANES)

    fwd, inv = tables(points, harmonics)
    entries = characteristic.transpose(0, 3, 4, 1, 2).reshape(-1, 2, harmonics)
    smem = pl.BlockSpec(memory_space=SMEM)
    anywhere = pl.BlockSpec(memory_space=pl.ANY)
    field_rows = cells * rows
    update = pl.pallas_call(
        lambda *refs: kernel(nv, axial, rows, cw, harmonics, *refs),
        out_shape=VMEM((nv * field_rows, LANES), F32),
        in_specs=[smem, smem] + [anywhere] * 6,
        out_specs=pl.BlockSpec(memory_space=VMEM),
        scratch_shapes=[
            VMEM((nv * field_rows, LANES), F32),
            VMEM((nv * field_rows, LANES), F32),
            VMEM((nn * field_rows, LANES), F32),
            VMEM(entries.shape, F32),
            VMEM(fwd.shape, BF16),
            VMEM(inv.shape, BF16),
            VMEM((2, cw * count, LANES), F32),
            VMEM((n, cw * count, LANES), F32),
            VMEM((rows, LANES), F32),
            VMEM((2, rows, LANES), F32),
            VMEM((2 * entries.shape[0], harmonics), F32),
            VMEM((4, 2 * nn, 2 * half, part), F32),
            VMEM((rows, nn, cells, LANES), F32),
            VMEM((rows, nn, cells, LANES), F32),
            VMEM((rows, nn, cells, LANES), F32),
            VMEM((nv * field_rows, LANES), F32),
            VMEM((rows, nv, cells, LANES), F32),
            VMEM((cells * EARLY, LANES), F32),
            VMEM((cells * PAIR, LANES), F32),
            VMEM((m, MAPS, LANES), F32),
            VMEM((m, EARLY, LANES), F32),
            VMEM((m, PAIR, LANES), F32),
            VMEM((m, PAIR, LANES), F32),
            VMEM((m, PAIR, LANES), F32),
            VMEM((cells * PAIR, LANES), F32),
            VMEM((cw * count, LANES), F32),
            VMEM((2, cw * count, LANES), F32),
            DMA((6,)),
            DMA((n - 1,)),
            DMA((n - 1,)),
            DMA((2,)),
            DMA((2,)),
            DMA,
            DMA,
            DMA((owners,)),
            DMA((m,)),
            DMA((owners,)),
            DMA((m,)),
            DMA((owners,)),
            DMA((m,)),
            DMA((m - 1,)),
            DMA((owners,)),
            DMA((m - 1,)),
            DMA((owners,)),
        ],
        compiler_params=pltpu.CompilerParams(collective_id=0, has_side_effects=True),
        name="step",
    )(
        cutoffs,
        coupling.reshape(-1),
        flat(residual),
        flat(prior),
        flat(inverse_diagonal),
        entries,
        jnp.asarray(fwd),
        jnp.asarray(inv),
    )
    update = update.reshape(nv, axial, cw, rows, LANES)
    return jnp.swapaxes(update, 2, 3).reshape(nv, axial, rows, width)


def solution(mesh):
    in_specs = (
        P(None, None, "span", "pitch"),
        P(None, None, None, "span", "pitch"),
        P(None, None, "span", "pitch"),
        P(),
        P(),
        P(),
    )
    out_specs = P(None, None, "span", "pitch")
    return jax.shard_map(body, mesh=mesh, in_specs=in_specs, out_specs=out_specs, check_vma=False)
```

time: 51 us -> 28 us (0.55)
  Pallas kernels: 37.2 us -> 25.7 us
  local copies, waits for them, and re-layouts: 11.5 us -> 2.07 us
  other arithmetic: 1.71 us -> 0 us
    pallas_call x2 -> x1, Pallas kernels: 37.2 us -> 25.7 us  [body(): pl.pallas_call(lambda *refs: kernel(nv, axial, rows, cw, harmonics, *refs...]
    reshape x9 -> x1, local copies, waits for them, and re-layouts: 6.38 us -> 0.67 us  [body(): coupling.reshape(-1)]
    transpose x4 -> x0, local copies, waits for them, and re-layouts: 1.81 us -> none  [the longest x3 1.79 us: by_row(): return jnp.moveaxis(field, -2, -3).reshape((-1, rows) + tile)]
    slice x9 -> x0, local copies, waits for them, and re-layouts: 1.07 us -> none  [the longest x2 0.38 us: edges_of(): return piece.reshape(-1)[:count].reshape(edge_shape)]
    scatter-add x2 -> x0, other arithmetic: 0.86 us -> none  [body(): residual.at[:, 0].add(correction[0]).at[:, -1].add(correction[1])]
    unnamed x13 -> x2, local copies, waits for them, and re-layouts: 2.18 us -> 1.4 us
    concatenate x1 -> x0, other arithmetic: 0.65 us -> none  [corrections(): jnp.concatenate([planes, edges])]
where the time goes in v1:
time: 28 us; the launch traced here: 27.8 us
  Pallas kernels  25.7 us (92%)
  local copies, waits for them, and re-layouts  2.07 us (7%)
    pallas_call x1, Pallas kernels, body(): pl.pallas_call(lambda *refs: kernel(nv, axial, rows, cw, harmonics, *refs...  25.7 us
    unnamed x2, local copies, waits for them, and re-layouts  1.4 us
    reshape x1, local copies, waits for them, and re-layouts, body(): coupling.reshape(-1)  0.67 us

profile of v1, /device:TPU:0, one launch (start us, length us, event | category | flops | bytes accessed | tf_op | source)
XLA Modules:
  0.0 27.8 jit_solution(6627920524525300256)
XLA Ops:
  0.0 0.7 %copy.9 = f32[6,5,5]{2,1,0:T(8,128)S(1)} copy(f32[6,5,5]{2,0,1:T(8,128)} %param.11) | data formatting | bytes 1200 | tf_op args[3]
  0.7 0.7 %reshape.30.refs_1_ = f32[150]{0:T(256)} reshape(f32[6,5,5]{2,1,0:T(8,128)S(1)} %copy.9) | data formatting | bytes 1200 | tf_op jit(solution)/shard_map/reshape | solution.py:651
  1.4 25.7 %step.1 = f32[320,128]{1,0:T(8,128)S(1)} custom-call(s32[2]{0:T(128)} %refs_0_.1, f32[150]{0:T(256)} %reshape.30.refs_1_, f32[320,128]{1,0:T(8,128)} %bitcast.26, f32[320,128]{1,0:T(8,128)} %bitcast.27, f32[1600,128]{1,0:T(8,128)} %bitcast.24, f32[50,2,512]{2,1,0:T(2,128)} %bitcast.25, bf16[2,256,1024]{2,1,0:T(8,128)(2,1)} %constant.4.clone.refs_6_, ...), custom_call_target="tpu_custom_call" | custom-call | tf_op jit(solution)/shard_map/step/pallas_call | solution.py:596
  27.1 0.7 %copy.11 = f32[5,4,8,256]{3,2,1,0:T(8,128)} copy(f32[5,4,8,256]{3,2,1,0:T(8,128)S(1)} %bitcast.23) | data formatting | bytes 327680

commit v2 on v1

--- a/solution.py
+++ b/solution.py
@@ -12,7 +12,6 @@
 SMEM = pltpu.SMEM
 DMA = pltpu.SemaphoreType.DMA
 MAPS = 80
-EARLY = 88
 PAIR = 16
 F32 = jnp.float32
 BF16 = jnp.bfloat16
@@ -73,16 +72,15 @@
 
 def kernel(
     nv, axial, rows, cw, harmonics,
-    cutoffs, coupling, res_in, prior_in, diag_in, char_in, fwd_in, inv_in,
+    cutoffs_in, coupling_in, res_in, prior_in, diag_in, char_in, fwd_in, inv_in,
     out,
-    res, prior, diag, char, fwd, inv,
+    cutoffs, coupling, res, prior, diag, char, fwd, inv,
     stage, lines, edge, edges, entries, chars,
-    low_steps, up_steps, grown, src, base, send_maps, send_pair,
-    got_late, got_early, got_pair, solved_early, solved_late, back,
+    low_steps, up_steps, grown, src, base, send_maps, send_first, send_pair,
+    got_late, got_early, got_first, got_pair, solved_early, solved_late, back,
     corr_send, corr_got,
-    in_sem, line_send, line_recv, edge_send, edge_recv, corr_ssem, corr_rsem,
-    late_send, late_recv, early_send, early_recv, pair_send, pair_recv,
-    re_send, re_recv, rl_send, rl_recv,
+    in_sem, sent, replied, lines_got, edges_got, swap_got,
+    late_got, early_got, first_got, pair_got, reply_got,
 ):
     n = lax.axis_size("pitch")
     m = lax.axis_size("span")
@@ -109,13 +107,13 @@
     copies = [
         pltpu.make_async_copy(a, b, in_sem.at[i])
         for i, (a, b) in enumerate(
-            [(res_in, res), (prior_in, prior), (diag_in, diag), (char_in, char),
-             (fwd_in, fwd), (inv_in, inv)]
+            [(res_in, res), (prior_in, prior), (diag_in, diag), (coupling_in, coupling),
+             (cutoffs_in, cutoffs), (char_in, char), (fwd_in, fwd), (inv_in, inv)]
         )
     ]
     for copy in copies:
         copy.start()
-    get_res, get_prior, get_diag, get_char, get_fwd, get_inv = copies
+    get_res, get_prior, get_diag, get_coupling, get_cutoffs, get_char, get_fwd, get_inv = copies
 
     barrier = pltpu.get_barrier_semaphore()
 
@@ -124,18 +122,24 @@
             barrier, inc=1, device_id={axis: to}, device_id_type=pl.DeviceIdType.MESH
         )
 
-    for step in range(1, n):
-        greet("pitch", lax.rem(me + step, n))
-
     @pl.when(is_owner)
     def _():
         for step in range(1, m):
-            greet("span", lax.rem(mine + step, m))
+            greet("span", jnp.bitwise_xor(mine, step))
 
     @pl.when(jnp.logical_not(is_owner))
     def _():
         for k in range(owners):
             greet("span", first + k)
+
+    for step in range(1, n):
+        greet("pitch", jnp.bitwise_xor(me, step))
+
+    def received(place, sem):
+        remote(place, place, sem, sem, {"pitch": jnp.bitwise_xor(me, 1)}).wait_recv()
+
+    def gone(place, sem):
+        remote(place, place, sem, sem, {"pitch": jnp.bitwise_xor(me, 1)}).wait_send()
 
     def tile(ref, i, a, c):
         at = ((i * axial + a) * cw + c) * rows
@@ -163,35 +167,8 @@
             packed = jnp.where(lane == nv * axial + at, right, packed)
     edge[...] = packed
 
-    @pl.when(is_owner)
-    def _():
-        pl.semaphore_wait(barrier, n - 1 + m - 1)
-
-    @pl.when(jnp.logical_not(is_owner))
-    def _():
-        pl.semaphore_wait(barrier, n - 1 + owners)
-
-    gather = []
-    for step in [s for s in range(2, n)] + [1]:
-        to = jnp.bitwise_xor(me, step)
-        gather.append(
-            remote(
-                stage.at[lax.rem(to, 2)], lines.at[me], line_send.at[step - 1],
-                line_recv.at[step - 1], {"pitch": to},
-            )
-        )
-        gather[-1].start()
-    after = lax.rem(me + 1, n)
-    before = lax.rem(me + n - 1, n)
-    edge_copies = [
-        remote(edge, edges.at[0], edge_send.at[0], edge_recv.at[0], {"pitch": after}),
-        remote(edge, edges.at[1], edge_send.at[1], edge_recv.at[1], {"pitch": before}),
-    ]
-    for copy in edge_copies:
-        copy.start()
-    lines[me] = stage[core]
-
     get_diag.wait()
+    get_coupling.wait()
     zero = jnp.zeros((cells, LANES), F32)
     one = jnp.ones((cells, LANES), F32)
     identity = [one if i == j else zero for j in range(nv) for i in range(nv)]
@@ -203,7 +180,7 @@
         return [[cell_row(diag, i * nv + j, row) for j in range(nv)] for i in range(nv)]
 
     def entry(which, i, j):
-        return coupling[(which * nv + i) * nv + j]
+        return coupling[i, which, j]
 
     def steps_at(ref, row):
         return [[ref[row, i * nv + j] for j in range(nv)] for i in range(nv)]
@@ -234,7 +211,25 @@
 
     last = lax.fori_loop(0, rows, grow, tuple(identity))
     for at in range(nn):
-        send_maps[pl.ds(at, cells, stride=EARLY), :] = last[at]
+        send_maps[pl.ds(at, cells, stride=MAPS), :] = last[at]
+
+    @pl.when(is_owner)
+    def _():
+        pl.semaphore_wait(barrier, n - 1 + m - 1)
+
+    @pl.when(jnp.logical_not(is_owner))
+    def _():
+        pl.semaphore_wait(barrier, n - 1 + owners)
+
+    after = lax.rem(me + 1, n)
+    before = lax.rem(me + n - 1, n)
+    remote(edge, edges.at[0], sent, edges_got, {"pitch": after}).start()
+    remote(edge, edges.at[1], sent, edges_got, {"pitch": before}).start()
+    for step in [s for s in range(2, n)] + [1]:
+        to = jnp.bitwise_xor(me, step)
+        remote(stage.at[lax.rem(to, 2)], lines.at[me], sent, lines_got, {"pitch": to}).start()
+    lines[me] = stage[core]
+
 
     def respond(index, carry):
         row = rows - 1 - index
@@ -243,14 +238,14 @@
 
     response = lax.fori_loop(0, rows, respond, tuple([zero] * nn))
     for at in range(nn):
-        send_maps[pl.ds(nn + at, cells, stride=EARLY), :] = response[at]
+        send_maps[pl.ds(nn + at, cells, stride=MAPS), :] = response[at]
 
     def shrink(index, carry):
         return tuple(advance(up_steps, rows - 1 - index, list(carry)))
 
     last = lax.fori_loop(0, rows, shrink, tuple(identity))
     for at in range(nn):
-        send_maps[pl.ds(2 * nn + at, cells, stride=EARLY), :] = last[at]
+        send_maps[pl.ds(2 * nn + at, cells, stride=MAPS), :] = last[at]
 
     def to_owners(make):
         for k in range(owners):
@@ -258,85 +253,23 @@
             def _(k=k):
                 make(k).start()
 
-    def late_copy(k):
-        return remote(
-            send_maps.at[pl.ds(late_row(k) * EARLY, MAPS), :], got_late.at[mine],
-            late_send.at[k], late_recv.at[mine], {"span": first + k},
+    def maps_copy(got, row, sem):
+        return lambda k: remote(
+            send_maps.at[pl.ds(row(k) * MAPS, 3 * nn), :], got.at[mine, pl.ds(0, 3 * nn), :],
+            sent, sem, {"span": first + k},
         )
 
-    def early_copy(k):
-        return remote(
-            send_maps.at[pl.ds(early_row(k) * EARLY, EARLY), :], got_early.at[mine],
-            early_send.at[k], early_recv.at[mine], {"span": first + k},
+    def ends_copy(send, got, row, sem):
+        return lambda k: remote(
+            send.at[pl.ds(row(k) * PAIR, 2 * nv), :], got.at[mine, pl.ds(0, 2 * nv), :],
+            sent, sem, {"span": first + k},
         )
 
-    def pair_copy(k):
-        return remote(
-            send_pair.at[pl.ds(late_row(k) * PAIR, PAIR), :], got_pair.at[mine],
-            pair_send.at[k], pair_recv.at[mine], {"span": first + k},
-        )
-
-    for copy in edge_copies:
-        copy.wait_recv()
-    from_left, from_right = edges[0], edges[1]
-    for a in range(axial):
-        for c in range(cw):
-            groups = [[], [], [], []]
-            for j in range(nv):
-                at = j * axial + a
-                here = tile(prior, j, a, c)
-                if c > 0:
-                    border = pltpu.roll(tile(prior, j, a, c - 1), 1, 1)
-                else:
-                    border = pltpu.roll(from_left, LANES - (nv * axial + at), 1)
-                groups[0].append(jnp.where(lane == 0, border, pltpu.roll(here, 1, 1)))
-                if c + 1 < cw:
-                    border = pltpu.roll(tile(prior, j, a, c + 1), LANES - 1, 1)
-                else:
-                    border = pltpu.roll(from_right, LANES - 1 - at, 1)
-                groups[1].append(
-                    jnp.where(lane == LANES - 1, border, pltpu.roll(here, LANES - 1, 1)))
-                if a > 0:
-                    groups[2].append(tile(prior, j, a - 1, c))
-                if a + 1 < axial:
-                    groups[3].append(tile(prior, j, a + 1, c))
-            for i in range(nv):
-                value = tile(res, i, a, c)
-                for side in range(4):
-                    for j, neighbour in enumerate(groups[side]):
-                        value = value - entry(2 + side, i, j) * neighbour
-                at = ((i * axial + a) * cw + c) * rows
-                src[at:at + rows, :] = value
-
-    def forward(row, star):
-        block = block_at(row)
-        rhs = [cell_row(src, i, row) for i in range(nv)]
-        known = times(block, rhs, nv)
-        for i in range(nv):
-            base[row, i] = known[i]
-        moved = times(steps_at(low_steps, row), list(star), nv)
-        star = [x + y for x, y in zip(known, moved)]
-        for i in range(nv):
-            grown[row, i] = star[i]
-        return tuple(star)
-
-    def backward(index, following):
-        row = rows - 1 - index
-        moved = times(steps_at(up_steps, row), list(following), nv)
-        return tuple(grown[row, i] + moved[i] for i in range(nv))
-
-    def local_sweeps():
-        last = lax.fori_loop(0, rows, forward, tuple([zero] * nv))
-        top = lax.fori_loop(0, rows, backward, tuple([zero] * nv))
-        return list(last) + list(top)
-
-    ends = local_sweeps()
-    for at in range(2 * nv):
-        send_maps[pl.ds(3 * nn + at, cells, stride=EARLY), :] = ends[at]
-    to_owners(late_copy)
-    to_owners(early_copy)
+    to_owners(maps_copy(got_late, late_row, late_got))
+    to_owners(maps_copy(got_early, early_row, early_got))
 
     get_char.wait()
+    get_cutoffs.wait()
     for at in range(2 * nn):
         entries[2 * at:2 * at + 2, :] = char[at]
     table = entries[...]
@@ -371,9 +304,65 @@
                                          (2 * half, part))
                     chars[s, 2 * (i * nv + j) + p] = jnp.where(upper, b, a) * weight
 
+    received(edges, edges_got)
+    from_left, from_right = edges[0], edges[1]
+    for a in range(axial):
+        for c in range(cw):
+            groups = [[], [], [], []]
+            for j in range(nv):
+                at = j * axial + a
+                here = tile(prior, j, a, c)
+                if c > 0:
+                    border = pltpu.roll(tile(prior, j, a, c - 1), 1, 1)
+                else:
+                    border = pltpu.roll(from_left, LANES - (nv * axial + at), 1)
+                groups[0].append(jnp.where(lane == 0, border, pltpu.roll(here, 1, 1)))
+                if c + 1 < cw:
+                    border = pltpu.roll(tile(prior, j, a, c + 1), LANES - 1, 1)
+                else:
+                    border = pltpu.roll(from_right, LANES - 1 - at, 1)
+                groups[1].append(
+                    jnp.where(lane == LANES - 1, border, pltpu.roll(here, LANES - 1, 1)))
+                if a > 0:
+                    groups[2].append(tile(prior, j, a - 1, c))
+                if a + 1 < axial:
+                    groups[3].append(tile(prior, j, a + 1, c))
+            for i in range(nv):
+                value = tile(res, i, a, c)
+                for side in range(4):
+                    for j, neighbour in enumerate(groups[side]):
+                        value = value - entry(2 + side, i, j) * neighbour
+                at = ((i * axial + a) * cw + c) * rows
+                src[at:at + rows, :] = value
+
+    def backward(following, row):
+        moved = times(steps_at(up_steps, row), following, nv)
+        return [grown[row, i] + moved[i] for i in range(nv)]
+
+    def local_sweeps(send):
+        star = None
+        for row in range(rows):
+            block = block_at(row)
+            known = times(block, [cell_row(src, i, row) for i in range(nv)], nv)
+            for i in range(nv):
+                base[row, i] = known[i]
+            if star is not None:
+                moved = times(steps_at(low_steps, row), star, nv)
+                known = [x + y for x, y in zip(known, moved)]
+            star = known
+            for i in range(nv):
+                grown[row, i] = star[i]
+        following = star
+        for row in reversed(range(rows - 1)):
+            following = backward(following, row)
+        for at, value in enumerate(star + following):
+            send[pl.ds(at, cells, stride=PAIR), :] = value
+
+    local_sweeps(send_first)
+    to_owners(ends_copy(send_first, got_first, early_row, first_got))
+
     get_fwd.wait()
-    for copy in gather:
-        copy.wait_recv()
+    received(lines.at[pl.ds(0, n - 1)], lines_got)
     per_quarter = (points // 4) // LANES
     quarters = []
     for q in range(4):
@@ -453,7 +442,7 @@
         corr_send[c * count:(c + 1) * count, :] = jnp.where(is_first, b, a)
         corr_got[0, c * count:(c + 1) * count, :] = jnp.where(is_first, a, b)
     swap = remote(
-        corr_send, corr_got.at[1], corr_ssem, corr_rsem, {"pitch": jnp.bitwise_xor(me, 1)})
+        corr_send, corr_got.at[1], sent, swap_got, {"pitch": jnp.bitwise_xor(me, 1)})
     swap.start()
     swap.wait_recv()
     lower_rows = lax.broadcasted_iota(jnp.int32, (rows, LANES), 0) < half
@@ -468,19 +457,17 @@
                 src[at:at + half, :] += jnp.where(is_first, ours, theirs)
                 src[at + half:at + rows, :] += jnp.where(is_first, theirs, ours)
 
-    ends = local_sweeps()
-    for at in range(2 * nv):
-        send_pair[pl.ds(at, cells, stride=PAIR), :] = ends[at]
-    to_owners(pair_copy)
-
-    def solve(maps, terms, offset, solved):
+    local_sweeps(send_pair)
+    to_owners(ends_copy(send_pair, got_pair, late_row, pair_got))
+
+    def solve(maps, terms, solved):
         def mapped(d, start, vector):
             return tree(
                 [maps[d, start + j * nv:start + (j + 1) * nv, :] * vector[j:j + 1]
                  for j in range(nv)])
 
         def term(d, which):
-            return terms[d, offset + which * nv:offset + (which + 1) * nv, :]
+            return terms[d, which * nv:(which + 1) * nv, :]
 
         incoming = jnp.zeros((nv, LANES), F32)
         every = []
@@ -496,24 +483,14 @@
                 known = term(d, 1) + mapped(d, nn, every[d])
                 following = known + mapped(d, 2 * nn, following)
 
-    def reply(solved, row, send, recv):
-        out_copies = []
+    def reply(solved, row):
+        place = back.at[pl.ds(pl.multiple_of(row * PAIR, 8), 2 * nv), :]
         for step in range(1, m):
-            to = lax.rem(mine + step, m)
-            out_copies.append(
-                remote(
-                    solved.at[to], back.at[pl.ds(pl.multiple_of(row * PAIR, 8), PAIR), :],
-                    send.at[step - 1], recv.at[own], {"span": to}))
-            out_copies[-1].start()
-        back[pl.ds(pl.multiple_of(row * PAIR, 8), PAIR), :] = solved[mine]
-        return out_copies
-
-    def arrived(make_buffer, recv):
-        for step in range(1, m):
-            d = lax.rem(mine + step, m)
+            to = jnp.bitwise_xor(mine, step)
             remote(
-                make_buffer.at[d], make_buffer.at[d], recv.at[d], recv.at[d], {"span": d}
-            ).wait_recv()
+                solved.at[to, pl.ds(0, 2 * nv), :], place, replied, reply_got, {"span": to}
+            ).start()
+        place[...] = solved[mine, 0:2 * nv, :]
 
     def own_rows(ref, row, stride, size):
         return ref[pl.ds(pl.multiple_of(row * stride, 8), size), :]
@@ -522,52 +499,48 @@
     def _():
         late = late_row(own)
         early = early_row(own)
-        got_early[mine] = own_rows(send_maps, early, EARLY, EARLY)
-        got_late[mine] = own_rows(send_maps, late, EARLY, MAPS)
+        got_early[mine] = own_rows(send_maps, early, MAPS, MAPS)
+        got_late[mine] = own_rows(send_maps, late, MAPS, MAPS)
+        got_first[mine] = own_rows(send_first, early, PAIR, PAIR)
         got_pair[mine] = own_rows(send_pair, late, PAIR, PAIR)
-        arrived(got_early, early_recv)
-        solve(got_early, got_early, 3 * nn, solved_early)
-        first_out = reply(solved_early, early, re_send, re_recv)
-        arrived(got_late, late_recv)
-        arrived(got_pair, pair_recv)
-        solve(got_late, got_pair, 0, solved_late)
-        second_out = reply(solved_late, late, rl_send, rl_recv)
-        for copy in first_out + second_out:
-            copy.wait_send()
-
-    for k in range(owners):
-        @pl.when(mine != first + k)
-        def _(k=k):
-            for row, recv in ((early_row(k), re_recv), (late_row(k), rl_recv)):
-                place = back.at[pl.ds(row * PAIR, PAIR), :]
-                remote(place, place, recv.at[k], recv.at[k], {"span": first + k}).wait_recv()
+        received(got_early.at[pl.ds(0, m - 1), pl.ds(0, 3 * nn), :], early_got)
+        received(got_first.at[pl.ds(0, m - 1), pl.ds(0, 2 * nv), :], first_got)
+        solve(got_early, got_first, solved_early)
+        reply(solved_early, early)
+        received(got_late.at[pl.ds(0, m - 1), pl.ds(0, 3 * nn), :], late_got)
+        received(got_pair.at[pl.ds(0, m - 1), pl.ds(0, 2 * nv), :], pair_got)
+        solve(got_late, got_pair, solved_late)
+        reply(solved_late, late)
+        gone(diag.at[pl.ds(0, 2 * (m - 1) * 2 * nv), :], replied)
+        received(diag.at[pl.ds(0, 2 * (owners - 1) * 2 * nv), :], reply_got)
+
+    @pl.when(jnp.logical_not(is_owner))
+    def _():
+        received(diag.at[pl.ds(0, 2 * owners * 2 * nv), :], reply_got)
 
     incoming = [back[pl.ds(i, cells, stride=PAIR), :] for i in range(2 * nv)]
-
-    def last_forward(row, star):
-        moved = times(steps_at(low_steps, row), list(star), nv)
+    star = incoming[:nv]
+    for row in range(rows):
+        moved = times(steps_at(low_steps, row), star, nv)
         star = [base[row, i] + moved[i] for i in range(nv)]
         for i in range(nv):
             grown[row, i] = star[i]
-        return tuple(star)
-
-    def last_backward(index, following):
-        row = rows - 1 - index
-        value = backward(index, following)
+    following = incoming[nv:]
+    for row in reversed(range(rows)):
+        following = backward(following, row)
         for i in range(nv):
-            out[pl.ds(i * cells * rows + row, cells, stride=rows), :] = value[i]
-        return value
-
-    lax.fori_loop(0, rows, last_forward, tuple(incoming[:nv]))
-    lax.fori_loop(0, rows, last_backward, tuple(incoming[nv:]))
-
-    for copy in gather + edge_copies + [swap]:
-        copy.wait_send()
-    for k in range(owners):
-        @pl.when(mine != first + k)
-        def _(k=k):
-            for make in (late_copy, early_copy, pair_copy):
-                make(k).wait_send()
+            out[pl.ds(i * cells * rows + row, cells, stride=rows), :] = following[i]
+
+    common = (n - 1) * cw * count + 2 * rows + cw * count
+    each = 2 * (3 * nn + 2 * nv)
+
+    @pl.when(is_owner)
+    def _():
+        gone(diag.at[pl.ds(0, common + (owners - 1) * each), :], sent)
+
+    @pl.when(jnp.logical_not(is_owner))
+    def _():
+        gone(diag.at[pl.ds(0, common + owners * each), :], sent)
 
 
 def body(residual, inverse_diagonal, prior, coupling, characteristic, cutoffs):
@@ -590,15 +563,16 @@
 
     fwd, inv = tables(points, harmonics)
     entries = characteristic.transpose(0, 3, 4, 1, 2).reshape(-1, 2, harmonics)
-    smem = pl.BlockSpec(memory_space=SMEM)
     anywhere = pl.BlockSpec(memory_space=pl.ANY)
     field_rows = cells * rows
     update = pl.pallas_call(
         lambda *refs: kernel(nv, axial, rows, cw, harmonics, *refs),
         out_shape=VMEM((nv * field_rows, LANES), F32),
-        in_specs=[smem, smem] + [anywhere] * 6,
+        in_specs=[anywhere] * 8,
         out_specs=pl.BlockSpec(memory_space=VMEM),
         scratch_shapes=[
+            SMEM((2,), jnp.int32),
+            SMEM((nv, 6, nv), F32),
             VMEM((nv * field_rows, LANES), F32),
             VMEM((nv * field_rows, LANES), F32),
             VMEM((nn * field_rows, LANES), F32),
@@ -616,39 +590,35 @@
             VMEM((rows, nn, cells, LANES), F32),
             VMEM((nv * field_rows, LANES), F32),
             VMEM((rows, nv, cells, LANES), F32),
-            VMEM((cells * EARLY, LANES), F32),
+            VMEM((cells * MAPS, LANES), F32),
+            VMEM((cells * PAIR, LANES), F32),
             VMEM((cells * PAIR, LANES), F32),
             VMEM((m, MAPS, LANES), F32),
-            VMEM((m, EARLY, LANES), F32),
+            VMEM((m, MAPS, LANES), F32),
+            VMEM((m, PAIR, LANES), F32),
             VMEM((m, PAIR, LANES), F32),
             VMEM((m, PAIR, LANES), F32),
             VMEM((m, PAIR, LANES), F32),
             VMEM((cells * PAIR, LANES), F32),
             VMEM((cw * count, LANES), F32),
             VMEM((2, cw * count, LANES), F32),
-            DMA((6,)),
-            DMA((n - 1,)),
-            DMA((n - 1,)),
-            DMA((2,)),
-            DMA((2,)),
-            DMA,
-            DMA,
-            DMA((owners,)),
-            DMA((m,)),
-            DMA((owners,)),
-            DMA((m,)),
-            DMA((owners,)),
-            DMA((m,)),
-            DMA((m - 1,)),
-            DMA((owners,)),
-            DMA((m - 1,)),
-            DMA((owners,)),
+            DMA((8,)),
+            DMA,
+            DMA,
+            DMA,
+            DMA,
+            DMA,
+            DMA,
+            DMA,
+            DMA,
+            DMA,
+            DMA,
         ],
         compiler_params=pltpu.CompilerParams(collective_id=0, has_side_effects=True),
         name="step",
     )(
         cutoffs,
-        coupling.reshape(-1),
+        coupling.transpose(1, 0, 2),
         flat(residual),
         flat(prior),
         flat(inverse_diagonal),

time: 28 us -> 20.9 us (0.75)
  Pallas kernels: 25.7 us -> 20.1 us
  local copies, waits for them, and re-layouts: 2.07 us -> 0.67 us
    pallas_call x1, Pallas kernels: 25.7 us -> 20.1 us  [body(): pl.pallas_call(lambda *refs: kernel(nv, axial, rows, cw, harmonics, *refs...]
    unnamed x2 -> x1, local copies, waits for them, and re-layouts: 1.4 us -> 0.67 us
    reshape x1 -> x0, local copies, waits for them, and re-layouts: 0.67 us -> none  [body(): coupling.reshape(-1)]
where the time goes in v2:
time: 20.9 us; the launch traced here: 20.8 us
  Pallas kernels  20.1 us (96%)
  local copies, waits for them, and re-layouts  0.67 us (3%)
    pallas_call x1, Pallas kernels, body(): pl.pallas_call(lambda *refs: kernel(nv, axial, rows, cw, harmonics, *refs...  20.1 us
    unnamed x1, local copies, waits for them, and re-layouts  0.67 us

profile of v2, /device:TPU:0, one launch (start us, length us, event | category | flops | bytes accessed | tf_op | source)
XLA Modules:
  0.0 20.8 jit_solution(6107661686029024323)
XLA Ops:
  0.0 20.1 %step.1 = f32[320,128]{1,0:T(8,128)S(1)} custom-call(s32[2]{0:T(128)} %refs_0_.1, f32[5,6,5]{2,1,0:T(8,128)} %bitcast.29, f32[320,128]{1,0:T(8,128)} %bitcast.27, f32[320,128]{1,0:T(8,128)} %bitcast.28, f32[1600,128]{1,0:T(8,128)} %bitcast.25, f32[50,2,512]{2,1,0:T(2,128)} %bitcast.26, bf16[2,256,1024]{2,1,0:T(8,128)(2,1)} %constant.4.clone.refs_6_, ...), custom_call_target="tpu_custom_call" | custom-call | tf_op jit(solution)/shard_map/step/pallas_call | solution.py:568
  20.1 0.7 %copy.10 = f32[5,4,8,256]{3,2,1,0:T(8,128)} copy(f32[5,4,8,256]{3,2,1,0:T(8,128)S(1)} %bitcast.24) | data formatting | bytes 327680

commit v3 on v2

--- a/solution.py
+++ b/solution.py
@@ -77,10 +77,10 @@
     cutoffs, coupling, res, prior, diag, char, fwd, inv,
     stage, lines, edge, edges, entries, chars,
     low_steps, up_steps, grown, src, base, send_maps, send_first, send_pair,
-    got_late, got_early, got_first, got_pair, solved_early, solved_late, back,
+    got_maps, got_first, got_pair, solved_early, solved_late, back,
     corr_send, corr_got,
     in_sem, sent, replied, lines_got, edges_got, swap_got,
-    late_got, early_got, first_got, pair_got, reply_got,
+    maps_got, first_got, pair_got, reply_got,
 ):
     n = lax.axis_size("pitch")
     m = lax.axis_size("span")
@@ -155,6 +155,20 @@
                     to = c * count + i * 2 * half + q * half
                     stage[h, to:to + half, :] = res[at:at + half, :]
 
+    @pl.when(is_owner)
+    def _():
+        pl.semaphore_wait(barrier, n - 1 + m - 1)
+
+    @pl.when(jnp.logical_not(is_owner))
+    def _():
+        pl.semaphore_wait(barrier, n - 1 + owners)
+
+    for step in [s for s in range(2, n)] + [1]:
+        to = jnp.bitwise_xor(me, step)
+        remote(stage.at[lax.rem(to, 2)], lines.at[me], sent, lines_got, {"pitch": to}).start()
+    lines[me] = stage[core]
+
+
     get_prior.wait()
     lane = lax.broadcasted_iota(jnp.int32, (rows, LANES), 1)
     packed = jnp.zeros((rows, LANES), F32)
@@ -167,106 +181,91 @@
             packed = jnp.where(lane == nv * axial + at, right, packed)
     edge[...] = packed
 
-    get_diag.wait()
-    get_coupling.wait()
-    zero = jnp.zeros((cells, LANES), F32)
-    one = jnp.ones((cells, LANES), F32)
-    identity = [one if i == j else zero for j in range(nv) for i in range(nv)]
-
-    def cell_row(ref, at, row):
-        return ref[pl.ds(at * cells * rows + row, cells, stride=rows), :]
-
-    def block_at(row):
-        return [[cell_row(diag, i * nv + j, row) for j in range(nv)] for i in range(nv)]
-
-    def entry(which, i, j):
-        return coupling[i, which, j]
-
-    def steps_at(ref, row):
-        return [[ref[row, i * nv + j] for j in range(nv)] for i in range(nv)]
-
-    def advance(ref, row, carry):
-        step = steps_at(ref, row)
-        new = []
-        for j in range(nv):
-            new += times(step, carry[j * nv:(j + 1) * nv], nv)
-        return new
-
-    def prepare(row, carry):
-        block = block_at(row)
-        for ref, which in ((low_steps, 0), (up_steps, 1)):
-            for k in range(nv):
-                column = [-entry(which, j, k) for j in range(nv)]
-                for i in range(nv):
-                    ref[row, i * nv + k] = tree([block[i][j] * column[j] for j in range(nv)])
-        return carry
-
-    lax.fori_loop(0, rows, prepare, 0)
-
-    def grow(row, carry):
-        new = advance(low_steps, row, list(carry))
-        for at in range(nn):
-            grown[row, at] = new[at]
-        return tuple(new)
-
-    last = lax.fori_loop(0, rows, grow, tuple(identity))
-    for at in range(nn):
-        send_maps[pl.ds(at, cells, stride=MAPS), :] = last[at]
-
-    @pl.when(is_owner)
-    def _():
-        pl.semaphore_wait(barrier, n - 1 + m - 1)
-
-    @pl.when(jnp.logical_not(is_owner))
-    def _():
-        pl.semaphore_wait(barrier, n - 1 + owners)
-
     after = lax.rem(me + 1, n)
     before = lax.rem(me + n - 1, n)
     remote(edge, edges.at[0], sent, edges_got, {"pitch": after}).start()
     remote(edge, edges.at[1], sent, edges_got, {"pitch": before}).start()
-    for step in [s for s in range(2, n)] + [1]:
-        to = jnp.bitwise_xor(me, step)
-        remote(stage.at[lax.rem(to, 2)], lines.at[me], sent, lines_got, {"pitch": to}).start()
-    lines[me] = stage[core]
-
-
-    def respond(index, carry):
-        row = rows - 1 - index
-        new = advance(up_steps, row, list(carry))
-        return tuple(grown[row, at] + new[at] for at in range(nn))
-
-    response = lax.fori_loop(0, rows, respond, tuple([zero] * nn))
-    for at in range(nn):
-        send_maps[pl.ds(nn + at, cells, stride=MAPS), :] = response[at]
-
-    def shrink(index, carry):
-        return tuple(advance(up_steps, rows - 1 - index, list(carry)))
-
-    last = lax.fori_loop(0, rows, shrink, tuple(identity))
-    for at in range(nn):
-        send_maps[pl.ds(2 * nn + at, cells, stride=MAPS), :] = last[at]
-
-    def to_owners(make):
+
+    get_diag.wait()
+    get_coupling.wait()
+
+    def cell_row(ref, at, row):
+        return ref[pl.ds(at * cells * rows + row, cells, stride=rows), :]
+
+    def block_at(row):
+        return [[cell_row(diag, i * nv + j, row) for j in range(nv)] for i in range(nv)]
+
+    def entry(which, i, j):
+        return coupling[i, which, j]
+
+    def steps_at(ref, row):
+        return [[ref[row, i * nv + j] for j in range(nv)] for i in range(nv)]
+
+    def product(step, columns):
+        result = []
+        for j in range(nv):
+            result += times(step, columns[j * nv:(j + 1) * nv], nv)
+        return result
+
+    def to_owners(make, sender=None):
         for k in range(owners):
-            @pl.when(mine != first + k)
+            other = mine != first + k
+            @pl.when(other if sender is None else jnp.logical_and(other, sender))
             def _(k=k):
                 make(k).start()
 
-    def maps_copy(got, row, sem):
+    is_last = mine == m - 1
+    is_inner = jnp.logical_and(mine > 0, mine < m - 1)
+
+    def store_maps(start, values):
+        for at, value in enumerate(values):
+            send_maps[pl.ds(start + at, cells, stride=MAPS), :] = value
+
+    def maps_copy(at, size):
         return lambda k: remote(
-            send_maps.at[pl.ds(row(k) * MAPS, 3 * nn), :], got.at[mine, pl.ds(0, 3 * nn), :],
-            sent, sem, {"span": first + k},
+            send_maps.reshape(axial // 2, 2, cw, MAPS, LANES).at[
+                k // cw, :, k % cw, pl.ds(at, size), :],
+            got_maps.reshape(m, 2, MAPS, LANES).at[mine, :, pl.ds(at, size), :],
+            sent, maps_got, {"span": first + k},
         )
+
+    growth = None
+    for row in range(rows):
+        block = block_at(row)
+        steps = []
+        for ref, which in ((low_steps, 0), (up_steps, 1)):
+            step = [[None] * nv for _ in range(nv)]
+            for k in range(nv):
+                column = [-entry(which, j, k) for j in range(nv)]
+                for i in range(nv):
+                    step[i][k] = tree([block[i][j] * column[j] for j in range(nv)])
+                    ref[row, i * nv + k] = step[i][k]
+            steps.append(step)
+        if growth is None:
+            growth = [steps[0][i][j] for j in range(nv) for i in range(nv)]
+        else:
+            growth = product(steps[0], growth)
+        for at in range(nn):
+            grown[row, at] = growth[at]
+    store_maps(0, growth)
+    to_owners(maps_copy(0, nn), is_inner)
+    response = growth
+    for row in reversed(range(rows - 1)):
+        moved = product(steps_at(up_steps, row), response)
+        response = [grown[row, at] + moved[at] for at in range(nn)]
+    step = steps_at(up_steps, rows - 1)
+    shrunk = [step[i][j] for j in range(nv) for i in range(nv)]
+    for row in reversed(range(rows - 1)):
+        shrunk = product(steps_at(up_steps, row), shrunk)
+    store_maps(nn, response + shrunk)
+    to_owners(maps_copy(nn, 2 * nn), is_inner)
+    to_owners(maps_copy(nn, nn), is_last)
 
     def ends_copy(send, got, row, sem):
         return lambda k: remote(
             send.at[pl.ds(row(k) * PAIR, 2 * nv), :], got.at[mine, pl.ds(0, 2 * nv), :],
             sent, sem, {"span": first + k},
         )
-
-    to_owners(maps_copy(got_late, late_row, late_got))
-    to_owners(maps_copy(got_early, early_row, early_got))
 
     get_char.wait()
     get_cutoffs.wait()
@@ -304,6 +303,90 @@
                                          (2 * half, part))
                     chars[s, 2 * (i * nv + j) + p] = jnp.where(upper, b, a) * weight
 
+    get_fwd.wait()
+    received(lines.at[pl.ds(0, n - 1)], lines_got)
+    per_quarter = (points // 4) // LANES
+    quarters = []
+    for q in range(4):
+        pieces = []
+        for t in range(q * per_quarter, (q + 1) * per_quarter):
+            d, c = t // cw, t % cw
+            pieces.append(lines[d, c * count:(c + 1) * count, :])
+        quarters.append(jnp.concatenate(pieces, axis=1))
+    even0, even1 = quarters[0] + quarters[2], quarters[1] + quarters[3]
+    odd0, odd1 = quarters[0] - quarters[2], quarters[1] - quarters[3]
+    wide = 2 * part
+
+    def onward(value, s):
+        return split_dot(
+            value, fwd[0, :, s * wide:(s + 1) * wide], fwd[1, :, s * wide:(s + 1) * wide])
+
+    real, imag = [None] * 4, [None] * 4
+    for s, value in ((0, even0 + even1), (2, even0 - even1)):
+        both = onward(value, s)
+        real[s], imag[s] = both[:, :part], -both[:, part:]
+    odd = jnp.concatenate([odd0, odd1])
+    both = onward(odd, 1)
+    real[1] = both[:count, :part] - both[count:, part:]
+    imag[1] = -(both[:count, part:] + both[count:, :part])
+    both = onward(odd, 3)
+    real[3] = both[:count, :part] + both[count:, part:]
+    imag[3] = both[count:, :part] - both[:count, part:]
+
+    new_real, new_imag = [], []
+    group = 2 * half
+    for s in range(4):
+        sr = [real[s][j * group:(j + 1) * group] for j in range(nv)]
+        si = [imag[s][j * group:(j + 1) * group] for j in range(nv)]
+        outr, outi = [], []
+        for i in range(nv):
+            cr = [chars[s, 2 * (i * nv + j)] for j in range(nv)]
+            ci = [chars[s, 2 * (i * nv + j) + 1] for j in range(nv)]
+            outr.append(total([cr[j] * sr[j] - ci[j] * si[j] for j in range(nv)]))
+            outi.append(total([cr[j] * si[j] + ci[j] * sr[j] for j in range(nv)]))
+        new_real.append(jnp.concatenate(outr))
+        new_imag.append(jnp.concatenate(outi))
+
+    get_inv.wait()
+
+    def homeward(value, s):
+        return split_dot(
+            value, inv[0, s * wide:(s + 1) * wide, :], inv[1, s * wide:(s + 1) * wide, :])
+
+    def beside(a, b):
+        return jnp.concatenate([a, b], axis=1)
+
+    r0 = homeward(beside(new_real[0], -new_imag[0]), 0)
+    r2 = homeward(beside(new_real[2], -new_imag[2]), 2)
+    both1 = homeward(
+        jnp.concatenate(
+            [beside(new_real[1], -new_imag[1]), beside(-new_imag[1], -new_real[1])]), 1)
+    both3 = homeward(
+        jnp.concatenate(
+            [beside(new_real[3], -new_imag[3]), beside(new_imag[3], new_real[3])]), 3)
+    odd_real = both1[:count] + both3[:count]
+    odd_imag = both1[count:] + both3[count:]
+    spans = (2 * cw) // per_quarter
+    if spans == 2:
+        sign = (1 - 2 * chip).astype(F32)
+        fields = [r0 + r2 + sign * odd_real, r0 - r2 + sign * odd_imag]
+    else:
+        sign = (1 - 2 * (chip // 2)).astype(F32)
+        turned = lax.rem(chip, 2).astype(F32)
+        straight = 1.0 - turned
+        field = r0 + (straight - turned) * r2 + sign * (
+            straight * odd_real + turned * odd_imag)
+        fields = [field[:, c * cw * LANES:(c + 1) * cw * LANES] for c in range(2)]
+    is_first = core == 0
+    for c in range(cw):
+        lo, hi = c * LANES, (c + 1) * LANES
+        a, b = fields[0][:, lo:hi], fields[1][:, lo:hi]
+        corr_send[c * count:(c + 1) * count, :] = jnp.where(is_first, b, a)
+        corr_got[0, c * count:(c + 1) * count, :] = jnp.where(is_first, a, b)
+    swap = remote(
+        corr_send, corr_got.at[1], sent, swap_got, {"pitch": jnp.bitwise_xor(me, 1)})
+    swap.start()
+
     received(edges, edges_got)
     from_left, from_right = edges[0], edges[1]
     for a in range(axial):
@@ -361,89 +444,6 @@
     local_sweeps(send_first)
     to_owners(ends_copy(send_first, got_first, early_row, first_got))
 
-    get_fwd.wait()
-    received(lines.at[pl.ds(0, n - 1)], lines_got)
-    per_quarter = (points // 4) // LANES
-    quarters = []
-    for q in range(4):
-        pieces = []
-        for t in range(q * per_quarter, (q + 1) * per_quarter):
-            d, c = t // cw, t % cw
-            pieces.append(lines[d, c * count:(c + 1) * count, :])
-        quarters.append(jnp.concatenate(pieces, axis=1))
-    even0, even1 = quarters[0] + quarters[2], quarters[1] + quarters[3]
-    odd0, odd1 = quarters[0] - quarters[2], quarters[1] - quarters[3]
-    wide = 2 * part
-
-    def onward(value, s):
-        return split_dot(
-            value, fwd[0, :, s * wide:(s + 1) * wide], fwd[1, :, s * wide:(s + 1) * wide])
-
-    real, imag = [None] * 4, [None] * 4
-    for s, value in ((0, even0 + even1), (2, even0 - even1)):
-        both = onward(value, s)
-        real[s], imag[s] = both[:, :part], -both[:, part:]
-    odd = jnp.concatenate([odd0, odd1])
-    both = onward(odd, 1)
-    real[1] = both[:count, :part] - both[count:, part:]
-    imag[1] = -(both[:count, part:] + both[count:, :part])
-    both = onward(odd, 3)
-    real[3] = both[:count, :part] + both[count:, part:]
-    imag[3] = both[count:, :part] - both[:count, part:]
-
-    new_real, new_imag = [], []
-    group = 2 * half
-    for s in range(4):
-        sr = [real[s][j * group:(j + 1) * group] for j in range(nv)]
-        si = [imag[s][j * group:(j + 1) * group] for j in range(nv)]
-        outr, outi = [], []
-        for i in range(nv):
-            cr = [chars[s, 2 * (i * nv + j)] for j in range(nv)]
-            ci = [chars[s, 2 * (i * nv + j) + 1] for j in range(nv)]
-            outr.append(total([cr[j] * sr[j] - ci[j] * si[j] for j in range(nv)]))
-            outi.append(total([cr[j] * si[j] + ci[j] * sr[j] for j in range(nv)]))
-        new_real.append(jnp.concatenate(outr))
-        new_imag.append(jnp.concatenate(outi))
-
-    get_inv.wait()
-
-    def homeward(value, s):
-        return split_dot(
-            value, inv[0, s * wide:(s + 1) * wide, :], inv[1, s * wide:(s + 1) * wide, :])
-
-    def beside(a, b):
-        return jnp.concatenate([a, b], axis=1)
-
-    r0 = homeward(beside(new_real[0], -new_imag[0]), 0)
-    r2 = homeward(beside(new_real[2], -new_imag[2]), 2)
-    both1 = homeward(
-        jnp.concatenate(
-            [beside(new_real[1], -new_imag[1]), beside(-new_imag[1], -new_real[1])]), 1)
-    both3 = homeward(
-        jnp.concatenate(
-            [beside(new_real[3], -new_imag[3]), beside(new_imag[3], new_real[3])]), 3)
-    odd_real = both1[:count] + both3[:count]
-    odd_imag = both1[count:] + both3[count:]
-    spans = (2 * cw) // per_quarter
-    if spans == 2:
-        sign = (1 - 2 * chip).astype(F32)
-        fields = [r0 + r2 + sign * odd_real, r0 - r2 + sign * odd_imag]
-    else:
-        sign = (1 - 2 * (chip // 2)).astype(F32)
-        turned = lax.rem(chip, 2).astype(F32)
-        straight = 1.0 - turned
-        field = r0 + (straight - turned) * r2 + sign * (
-            straight * odd_real + turned * odd_imag)
-        fields = [field[:, c * cw * LANES:(c + 1) * cw * LANES] for c in range(2)]
-    is_first = core == 0
-    for c in range(cw):
-        lo, hi = c * LANES, (c + 1) * LANES
-        a, b = fields[0][:, lo:hi], fields[1][:, lo:hi]
-        corr_send[c * count:(c + 1) * count, :] = jnp.where(is_first, b, a)
-        corr_got[0, c * count:(c + 1) * count, :] = jnp.where(is_first, a, b)
-    swap = remote(
-        corr_send, corr_got.at[1], sent, swap_got, {"pitch": jnp.bitwise_xor(me, 1)})
-    swap.start()
     swap.wait_recv()
     lower_rows = lax.broadcasted_iota(jnp.int32, (rows, LANES), 0) < half
     for c in range(cw):
@@ -460,26 +460,26 @@
     local_sweeps(send_pair)
     to_owners(ends_copy(send_pair, got_pair, late_row, pair_got))
 
-    def solve(maps, terms, solved):
+    def solve(slot, terms, solved):
         def mapped(d, start, vector):
+            at = pl.multiple_of((2 * d + slot) * MAPS, 8) + start
             return tree(
-                [maps[d, start + j * nv:start + (j + 1) * nv, :] * vector[j:j + 1]
-                 for j in range(nv)])
+                [got_maps[pl.ds(at + j * nv, nv), :] * vector[j:j + 1] for j in range(nv)])
 
         def term(d, which):
             return terms[d, which * nv:(which + 1) * nv, :]
 
-        incoming = jnp.zeros((nv, LANES), F32)
-        every = []
-        for d in range(m):
-            every.append(incoming)
-            solved[d, 0:nv, :] = incoming
-            if d + 1 < m:
-                incoming = term(d, 0) + mapped(d, 0, incoming)
-        following = jnp.zeros((nv, LANES), F32)
+        none = jnp.zeros((nv, LANES), F32)
+        every = [none, term(0, 0)]
+        for d in range(1, m - 1):
+            every.append(term(d, 0) + mapped(d, 0, every[d]))
+        following = none
         for d in reversed(range(m)):
+            solved[d, 0:nv, :] = every[d]
             solved[d, nv:2 * nv, :] = following
-            if d > 0:
+            if d == m - 1:
+                following = term(d, 1) + mapped(d, nn, every[d])
+            elif d > 0:
                 known = term(d, 1) + mapped(d, nn, every[d])
                 following = known + mapped(d, 2 * nn, following)
 
@@ -499,17 +499,19 @@
     def _():
         late = late_row(own)
         early = early_row(own)
-        got_early[mine] = own_rows(send_maps, early, MAPS, MAPS)
-        got_late[mine] = own_rows(send_maps, late, MAPS, MAPS)
+        side = own // cw
+        for slot in range(2):
+            row = (2 * side + slot) * cw + lax.rem(own, cw)
+            place = pl.ds(pl.multiple_of((2 * mine + slot) * MAPS, 8), MAPS)
+            got_maps[place, :] = own_rows(send_maps, row, MAPS, MAPS)
         got_first[mine] = own_rows(send_first, early, PAIR, PAIR)
         got_pair[mine] = own_rows(send_pair, late, PAIR, PAIR)
-        received(got_early.at[pl.ds(0, m - 1), pl.ds(0, 3 * nn), :], early_got)
+        received(got_maps.at[pl.ds(0, 2 * ((m - 3) * 3 * nn + nn)), :], maps_got)
         received(got_first.at[pl.ds(0, m - 1), pl.ds(0, 2 * nv), :], first_got)
-        solve(got_early, got_first, solved_early)
+        solve(1 - side, got_first, solved_early)
         reply(solved_early, early)
-        received(got_late.at[pl.ds(0, m - 1), pl.ds(0, 3 * nn), :], late_got)
         received(got_pair.at[pl.ds(0, m - 1), pl.ds(0, 2 * nv), :], pair_got)
-        solve(got_late, got_pair, solved_late)
+        solve(side, got_pair, solved_late)
         reply(solved_late, late)
         gone(diag.at[pl.ds(0, 2 * (m - 1) * 2 * nv), :], replied)
         received(diag.at[pl.ds(0, 2 * (owners - 1) * 2 * nv), :], reply_got)
@@ -538,9 +540,14 @@
     def _():
         gone(diag.at[pl.ds(0, common + (owners - 1) * each), :], sent)
 
-    @pl.when(jnp.logical_not(is_owner))
-    def _():
-        gone(diag.at[pl.ds(0, common + owners * each), :], sent)
+    for sender, size in (
+        (jnp.logical_and(is_inner, jnp.logical_not(is_owner)), each),
+        (mine == 0, each - 2 * 3 * nn),
+        (is_last, each - 2 * (3 * nn - nn)),
+    ):
+        @pl.when(sender)
+        def _(size=size):
+            gone(diag.at[pl.ds(0, common + owners * size), :], sent)
 
 
 def body(residual, inverse_diagonal, prior, coupling, characteristic, cutoffs):
@@ -593,8 +600,7 @@
             VMEM((cells * MAPS, LANES), F32),
             VMEM((cells * PAIR, LANES), F32),
             VMEM((cells * PAIR, LANES), F32),
-            VMEM((m, MAPS, LANES), F32),
-            VMEM((m, MAPS, LANES), F32),
+            VMEM((2 * m * MAPS, LANES), F32),
             VMEM((m, PAIR, LANES), F32),
             VMEM((m, PAIR, LANES), F32),
             VMEM((m, PAIR, LANES), F32),
@@ -603,7 +609,6 @@
             VMEM((cw * count, LANES), F32),
             VMEM((2, cw * count, LANES), F32),
             DMA((8,)),
-            DMA,
             DMA,
             DMA,
             DMA,

time: 20.9 us -> 20.3 us (0.971)
  Pallas kernels: 20.1 us -> 19.5 us
    pallas_call x1, Pallas kernels: 20.1 us -> 19.5 us  [body(): pl.pallas_call(lambda *refs: kernel(nv, axial, rows, cw, harmonics, *refs...]
where the time goes in v3:
time: 20.3 us; the launch traced here: 20.2 us
  Pallas kernels  19.5 us (96%)
  local copies, waits for them, and re-layouts  0.67 us (3%)
    pallas_call x1, Pallas kernels, body(): pl.pallas_call(lambda *refs: kernel(nv, axial, rows, cw, harmonics, *refs...  19.5 us
    unnamed x1, local copies, waits for them, and re-layouts  0.67 us

profile of v3, /device:TPU:0, one launch (start us, length us, event | category | flops | bytes accessed | tf_op | source)
XLA Modules:
  0.0 20.2 jit_solution(12263670094032638001)
XLA Ops:
  0.0 19.5 %step.1 = f32[320,128]{1,0:T(8,128)S(1)} custom-call(s32[2]{0:T(128)} %refs_0_.1, f32[5,6,5]{2,1,0:T(8,128)} %bitcast.29, f32[320,128]{1,0:T(8,128)} %bitcast.27, f32[320,128]{1,0:T(8,128)} %bitcast.28, f32[1600,128]{1,0:T(8,128)} %bitcast.25, f32[50,2,512]{2,1,0:T(2,128)} %bitcast.26, bf16[2,256,1024]{2,1,0:T(8,128)(2,1)} %constant.4.clone.refs_6_, ...), custom_call_target="tpu_custom_call" | custom-call | tf_op jit(solution)/shard_map/step/pallas_call | solution.py:575
  19.5 0.7 %copy.10 = f32[5,4,8,256]{3,2,1,0:T(8,128)} copy(f32[5,4,8,256]{3,2,1,0:T(8,128)S(1)} %bitcast.24) | data formatting | bytes 327680
